TPU v7x, 32 devices: a whole 2x2x4 slice. The times are simulated.
32 devices in a mesh: mem: 2 (over y), space: 16 (over z, x, core).
Axes of the slice: x: 2, y: 2, z: 4, core: 2. Of those that a mesh axis runs over, the one named last changes fastest.
Arguments:
- ensemble: bfloat16 [64, 160, 32, 128], P('mem', None, 'space'), may hold values from -6 to 6
- obs_value: float32 [16, 256], P('space'), may hold values from -6 to 6
- obs_error: float32 [16, 256], P('space'), may hold values from 0.3 to 3
- obs_cell: int32 [16, 256], P('space'), may hold values from 0 to 255
- obs_species: int32 [16, 256], P('space'), may hold values from 0 to 39
- patch_index: int32 [16, 256, 32], P('space', 'mem'), may hold values from 0 to 767, as said below
- patch_count: int32 [16, 256], P('space', 'mem'), may hold values from 1 to 32, as said below
- courant_x: float32 [4, 32, 128], P(None, 'space'), may hold values from -0.7 to 0.7
- courant_y: float32 [4, 32, 128], P(None, 'space'), may hold values from -0.7 to 0.7
- dep_velocity: float32 [40], replicated, may hold values from 0.05 to 0.5
- surface_factor: float32 [32, 128], P('space'), may hold values from 0.5 to 2
Outputs:
- forecast: bfloat16 [64, 160, 32, 128], P('mem', None, 'space')
Inputs may be any that keep to these rules, and one draw needn't show every extreme that they name: `patch_index`: each cell's list names distinct pool observations of existing tiles, nearest to the cell first; those within 3 cells of the cell come first. `patch_count`: the number of listed observations used for the cell, at least 1 and at most 32; the most is reached in every draw.
All inputs are finite; a program needn't handle non-finite values.
Results may differ from a plain program's by a relative error of at most 0.0049.
Values may be sent and summed in bfloat16 or wider, within the bound.
A program may use at most 64 MiB of HBM per device.

v0:
```python
import functools
import math

import jax
import jax.numpy as jnp
from jax import lax
from jax.experimental import pallas as pl
from jax.experimental.pallas import tpu as pltpu
from jax.sharding import PartitionSpec as P

NEWTON = 8
SUBSTEPS = 2
LOC = 1
LANES = 128
GROUP = 8
PITCH = 40
INTERPRET = False


def lane_product(left, right, depth, rows, width, finish, unroll=4):
    def group(block, carry):
        first = pl.multiple_of(block * GROUP, GROUP)

        def step(k, sums):
            row = right(k)
            return tuple(sums[r] + left(k, first, r) * row for r in range(GROUP))

        zero = jnp.zeros((width, LANES), jnp.float32)
        sums = lax.fori_loop(0, depth, step, (zero,) * GROUP, unroll=unroll)
        finish(first, sums)
        return carry

    lax.fori_loop(0, rows // GROUP, group, 0)


def weights_kernel(
    members, repeats, radius,
    pool_ref, idx_ref, cnt_ref, row_ref, col_ref,
    dev_ref, mix_ref, keep_ref,
    first_v, now_v, step_g, keys, tail, innov, scal,
):
    slots = idx_ref.shape[0]
    pooled = pool_ref.shape[1]
    blocks = slots // GROUP
    info = pool_ref[members:, :]
    high = info.astype(jnp.bfloat16).astype(jnp.float32)
    rest = info - high
    middle = rest.astype(jnp.bfloat16).astype(jnp.float32)
    low = rest - middle
    table = jnp.concatenate([pool_ref[:members, :], high, middle, low, jnp.zeros_like(low)], axis=0)
    table = table.astype(jnp.bfloat16)
    place = lax.broadcasted_iota(jnp.int32, (pooled, LANES), 0)
    extra = info.shape[0]

    def pick(k, total):
        hot = jnp.where(place == idx_ref[pl.ds(k, 1), :], 1.0, 0.0).astype(jnp.bfloat16)
        got = jnp.dot(table, hot, preferred_element_type=jnp.float32)
        equiv = got[:members]
        facts = (
            got[members : members + extra]
            + got[members + extra : members + 2 * extra]
            + got[members + 2 * extra : members + 3 * extra]
        )
        mean = jnp.sum(equiv, axis=0, keepdims=True) * (1.0 / members)
        dist = (facts[2:3] - row_ref[...]) ** 2 + (facts[3:4] - col_ref[...]) ** 2
        rho = jnp.exp(-dist / (2.0 * radius * radius)) / facts[1:2]
        scale = jnp.sqrt(jnp.where(k < cnt_ref[...], rho, 0.0))
        scaled = (equiv - mean) * scale
        dev_ref[pl.ds(k, members, stride=slots), :] = scaled
        innov[pl.ds(k, 1), :] = (facts[0:1] - mean) * scale
        return total + jnp.sum(scaled * scaled, axis=0, keepdims=True)

    spread = lax.fori_loop(0, slots, pick, jnp.zeros((1, LANES), jnp.float32), unroll=2)
    shift = members - 1.0
    inverse = 1.0 / (spread + shift * members)
    level = lax.broadcasted_iota(jnp.int32, (GROUP, LANES), 0)

    def eye(r, value):
        return jnp.where(level == r, value, 0.0)

    def at(ref, i, j, base=0):
        start = i * PITCH + j * GROUP
        start = start if isinstance(start, int) else pl.multiple_of(start, GROUP)
        return ref[pl.ds(base + start, GROUP), :]

    def put(ref, i, parts, base=0):
        for j, part in enumerate(parts):
            ref[pl.ds(base + i * PITCH + j * GROUP, GROUP), :] = part
            if j < i // GROUP:
                ref[pl.ds(base + j * GROUP * PITCH + i, GROUP, stride=PITCH), :] = part

    def product(left, right, depth, finish, unroll=4):
        for pair in range((blocks + 1) // 2):
            groups = sorted({pair, blocks - 1 - pair})

            def step(k, sums):
                wide = [right(k, j) for j in range(groups[-1] + 1)]
                out, spot = [], 0
                for g in groups:
                    for r in range(GROUP):
                        one = left(k, g * GROUP + r)
                        for j in range(g + 1):
                            out.append(sums[spot] + one * wide[j])
                            spot += 1
                return tuple(out)

            zero = jnp.zeros((GROUP, LANES), jnp.float32)
            count = sum((g + 1) * GROUP for g in groups)
            sums = lax.fori_loop(0, depth, step, (zero,) * count, unroll=unroll)
            spot = 0
            for g in groups:
                for r in range(GROUP):
                    finish(g * GROUP + r, sums[spot : spot + g + 1])
                    spot += g + 1

    def square(left, right, finish, left_base=0):
        product(
            lambda k, i: left[pl.ds(left_base + k * PITCH + i, 1), :],
            lambda k, j: at(right, k, j),
            slots, finish,
        )

    def gram_done(i, sums):
        parts = [part * inverse for part in sums]
        put(first_v, i, parts)
        put(now_v, i, parts)

    product(
        lambda k, i: dev_ref[pl.ds(k * slots + i, 1), :],
        lambda k, j: dev_ref[pl.ds(pl.multiple_of(k * slots, slots) + j * GROUP, GROUP), :],
        members, gram_done,
    )

    xi = shift * inverse
    mus = []
    for k in range(repeats):
        mu = 1.5 - 0.5 * xi
        scal[pl.ds(k, 1), :] = xi
        scal[pl.ds(repeats + k, 1), :] = mu
        mus.append(mu)
        xi = xi * mu * mu
    after = mus[-1]
    for k in reversed(range(repeats - 1)):
        scal[pl.ds(2 * repeats + k, 1), :] = after
        after = after * mus[k]
    last_z = after
    area = slots * PITCH

    def forward(n, carry):
        xi = scal[pl.ds(n, 1), :]
        mu = scal[pl.ds(repeats + n, 1), :]
        flat, slope = mu * mu - xi * mu, 0.25 * xi - mu
        base = pl.multiple_of(n * area, GROUP)

        def to_g(i, sums):
            parts = [0.25 * part + slope * at(now_v, i, j) for j, part in enumerate(sums)]
            parts[-1] = parts[-1] + eye(i % GROUP, flat)
            put(step_g, i, parts)

        square(now_v, now_v, to_g)

        def to_v(i, sums):
            put(tail, i, sums)
            put(keys, i, [mu * at(step_g, i, j) - 0.5 * part for j, part in enumerate(sums)], base)

        square(step_g, now_v, to_v)
        now_v[...] = tail[...]
        return carry

    lax.fori_loop(0, repeats - 1, forward, 0)

    after = scal[pl.ds(3 * repeats - 2, 1), :]
    for i in range(slots):
        parts = [-0.5 * at(keys, i, j, (repeats - 2) * area) for j in range(blocks)]
        parts[i // GROUP] = parts[i // GROUP] - eye(i % GROUP, 0.5 * after)
        for j, part in enumerate(parts):
            now_v[pl.ds(i * PITCH + j * GROUP, GROUP), :] = part

    def backward(m, carry):
        n = repeats - 3 - m
        base = pl.multiple_of(n * area, GROUP)
        half = 0.5 * scal[pl.ds(2 * repeats + n, 1), :]

        def to_h(i, sums):
            parts = list(sums)
            parts[-1] = parts[-1] - eye(i % GROUP, half)
            put(tail, i, parts)

        square(keys, now_v, to_h, base)
        now_v[...] = tail[...]
        return carry

    lax.fori_loop(0, repeats - 2, backward, 0)

    def whole(ref, k):
        return ref[pl.ds(pl.multiple_of(k * PITCH, GROUP), slots), :]

    none = jnp.zeros((slots, LANES), jnp.float32)

    def apply(ref):
        def step(k, total):
            return total + innov[pl.ds(k, 1), :] * whole(ref, k)

        return lax.fori_loop(0, slots, step, none)

    for _ in range(2):
        start = innov[...]
        innov[...] = apply(now_v)
        innov[...] = last_z * start + apply(first_v)
    gain = innov[...] * inverse
    factor = math.sqrt(shift) * jnp.sqrt(inverse)
    keep_ref[...] = factor * last_z
    both = factor * inverse

    def to_mix(first, sums):
        for r in range(GROUP):
            mix_ref[pl.ds(pl.multiple_of((first + r) * slots, slots), slots), :] = both * sums[r] + gain

    lane_product(
        lambda k, first, r: dev_ref[pl.ds((first + r) * slots + k, 1), :],
        lambda k: whole(now_v, k), slots, members, slots, to_mix,
    )


def solve_cells(pool, idx, counts, rows, cols, members):
    slots, cells = idx.shape
    lane = lambda height: pl.BlockSpec((height, LANES), lambda c: (0, c))
    square = pltpu.VMEM((slots * PITCH, LANES), jnp.float32)
    return pl.pallas_call(
        functools.partial(weights_kernel, members, NEWTON, LOC),
        grid=(cells // LANES,),
        in_specs=[pl.BlockSpec(pool.shape, lambda c: (0, 0)), lane(slots), lane(1), lane(1), lane(1)],
        out_specs=[lane(members * slots), lane(members * slots), lane(1)],
        out_shape=[
            jax.ShapeDtypeStruct((members * slots, cells), jnp.float32),
            jax.ShapeDtypeStruct((members * slots, cells), jnp.float32),
            jax.ShapeDtypeStruct((1, cells), jnp.float32),
        ],
        scratch_shapes=[square] * 3 + [
            pltpu.VMEM(((NEWTON - 1) * slots * PITCH, LANES), jnp.float32),
            square,
            pltpu.VMEM((slots, LANES), jnp.float32),
            pltpu.VMEM((3 * NEWTON, LANES), jnp.float32),
        ],
        compiler_params=pltpu.CompilerParams(vmem_limit_bytes=40 * 1024 * 1024),
        cost_estimate=pl.CostEstimate(flops=2 * 10**9, bytes_accessed=200 * 10**6, transcendentals=0),
        interpret=INTERPRET,
    )(pool, idx, counts, rows, cols)


def prep_kernel(rows, ens_ref, small_ref, pool_ref, edge_ref, mine_ref, theirs_ref, block, land, spread, send_sems, recv_sems):
    share, fields, _ = mine_ref.shape
    observed = small_ref.shape[1]
    span = fields * rows
    facts = small_ref.shape[0]
    me, place, count = lax.axis_index("mem"), lax.axis_index("space"), lax.axis_size("space")

    def exists(step):
        return (place + step >= 0) & (place + step < count)

    def guard(step, act):
        if step == 0:
            act()
        else:
            pl.when(exists(step))(act)

    ways = [(1, 0), (0, -1), (0, 1), (1, -1), (1, 1)]
    barrier = pltpu.get_barrier_semaphore()

    def target(flip, step):
        return (1 - me if flip else me, place + step)

    for flip, step in ways:
        def greet(flip=flip, step=step):
            pl.semaphore_signal(barrier, inc=1, device_id=target(flip, step), device_id_type=pl.DeviceIdType.MESH)

        guard(step, greet)

    block[pl.ds(share, facts), :] = small_ref[...]
    hot = jnp.where(
        lax.broadcasted_iota(jnp.int32, (LANES, observed), 0).astype(jnp.float32) == small_ref[3:4, :], 1.0, 0.0
    ).astype(jnp.bfloat16)
    wanted = lax.broadcasted_iota(jnp.int32, (span, observed), 0).astype(jnp.float32) == small_ref[4:5, :]

    def look(i, carry):
        got = jnp.dot(
            ens_ref[pl.ds(pl.multiple_of(i * span, span), span), :], hot, preferred_element_type=jnp.float32
        )
        block[pl.ds(i, 1), :] = jnp.sum(jnp.where(wanted, got, 0.0), axis=0, keepdims=True)
        return carry

    lax.fori_loop(0, share, look, 0)

    greeted = 1 + 2 * exists(-1).astype(jnp.int32) + 2 * exists(1).astype(jnp.int32)
    pl.semaphore_wait(barrier, greeted)

    def copy(n):
        flip, step = ways[n]
        return pltpu.make_async_remote_copy(
            src_ref=block, dst_ref=land.at[1 - step, flip],
            send_sem=send_sems.at[n], recv_sem=recv_sems.at[1 - step, flip],
            device_id=target(flip, step), device_id_type=pl.DeviceIdType.MESH,
        )

    for n, (flip, step) in enumerate(ways):
        guard(step, lambda n=n: copy(n).start())

    def split(pair, carry):
        for slot in range(2):
            i = 2 * pair + slot
            spread[slot] = ens_ref[pl.ds(pl.multiple_of(i * span, span), span), :].astype(jnp.float32)
            mine_ref[i] = spread[slot, pl.ds(me, fields, stride=rows), :].astype(jnp.bfloat16)
            theirs_ref[i] = spread[slot, pl.ds(1 - me, fields, stride=rows), :].astype(jnp.bfloat16)
        return carry

    lax.fori_loop(0, share // 2, split, 0)

    for n, (flip, step) in enumerate(ways):
        def arrive(n=n):
            copy(n).wait_send()

        guard(step, arrive)
    for n, (flip, step) in enumerate(ways):
        def landed(n=n):
            copy(n).wait_recv()

        guard(-step, landed)
    for step in (-1, 1):
        def blank(step=step):
            land[1 + step] = jnp.zeros_like(land[1 + step])

        pl.when(jnp.logical_not(exists(step)))(blank)
    line = lax.broadcasted_iota(jnp.int32, (GROUP, observed), 0)
    for part in range(3):
        own = block[...] if part == 1 else land[part, 0]
        lanes = pl.ds(part * observed, observed)
        pool_ref[pl.ds(0, share), lanes] = own[:share]
        pool_ref[pl.ds(share, share), lanes] = land[part, 1, pl.ds(0, share), :]
        pool_ref[pl.ds(2 * share, GROUP), lanes] = own[share : share + GROUP] + jnp.where(
            line == 2, float(rows * (part - 1)), 0.0
        )
        edge_ref[part] = own[share + GROUP :]


def prepare(flat, small, members, fields, rows):
    share = members // 2
    observed = small.shape[1]
    high = share + small.shape[0]
    vmem = pl.BlockSpec(memory_space=pltpu.VMEM)
    return pl.pallas_call(
        functools.partial(prep_kernel, rows),
        in_specs=[vmem] * 2,
        out_specs=[vmem] * 4,
        out_shape=[
            jax.ShapeDtypeStruct((members + GROUP, 3 * observed), jnp.float32),
            jax.ShapeDtypeStruct((3, small.shape[0] - GROUP, observed), jnp.float32),
            jax.ShapeDtypeStruct((share, fields, LANES), jnp.bfloat16),
            jax.ShapeDtypeStruct((share, fields, LANES), jnp.bfloat16),
        ],
        scratch_shapes=[
            pltpu.VMEM((high, observed), jnp.float32),
            pltpu.VMEM((3, 2, high, observed), jnp.float32),
            pltpu.VMEM((2, fields * rows, LANES), jnp.float32),
            pltpu.SemaphoreType.DMA((5,)),
            pltpu.SemaphoreType.DMA((3, 2)),
        ],
        compiler_params=pltpu.CompilerParams(
            vmem_limit_bytes=32 * 1024 * 1024, collective_id=0, has_side_effects=True
        ),
        cost_estimate=pl.CostEstimate(flops=10**8, bytes_accessed=8 * 10**6, transcendentals=0),
        interpret=INTERPRET,
    )(flat, small)


def analysis_kernel(parts, slots, *refs):
    states = refs[:parts]
    dev_ref, mix_ref, keep_ref = refs[parts : parts + 3]
    outs = refs[parts + 3 : 2 * parts + 3]
    anomaly, mapped, mean_ref = refs[2 * parts + 3 :]
    share, width, _ = states[0].shape
    members = share * parts
    total = jnp.zeros((width, LANES), jnp.float32)
    for state in states:
        total = lax.fori_loop(
            0, share, lambda i, t, s=state: t + s[i].astype(jnp.float32), total, unroll=4
        )
    mean = total * (1.0 / members)
    mean_ref[...] = mean
    for part, state in enumerate(states):

        def subtract(i, carry, s=state, base=part * share):
            anomaly[base + i] = s[i].astype(jnp.float32) - mean_ref[...]
            return carry

        lax.fori_loop(0, share, subtract, 0, unroll=4)

    def to_mapped(first, sums):
        for r in range(GROUP):
            mapped[first + r] = sums[r]

    lane_product(
        lambda i, first, r: dev_ref[pl.ds(i * slots + first + r, 1), :],
        lambda i: anomaly[i], members, slots, width, to_mapped,
    )
    for part, out in enumerate(outs):
        base = part * share

        def to_out(first, sums, out=out, base=base):
            for r in range(GROUP):
                held = mean_ref[...] + keep_ref[...] * anomaly[base + first + r]
                out[first + r] = (held + sums[r]).astype(jnp.bfloat16)

        lane_product(
            lambda k, first, r, base=base: mix_ref[pl.ds((base + first + r) * slots + k, 1), :],
            lambda k: mapped[k], slots, share, width, to_out,
        )


def analyse(states, dev, mix, keep, slots, first, count, width):
    share, _, cells = states[0].shape
    parts = len(states)
    members = share * parts
    wide = lambda height: pl.BlockSpec((height, LANES), lambda c, f: (0, c))
    return pl.pallas_call(
        functools.partial(analysis_kernel, parts, slots),
        grid=(cells // LANES, count // width),
        in_specs=[
            pl.BlockSpec((share, width, LANES), lambda c, f: (0, f + first // width, c))
        ] * parts + [wide(members * slots), wide(members * slots), wide(1)],
        out_specs=[pl.BlockSpec((share, width, LANES), lambda c, f: (0, f, c))] * parts,
        out_shape=[jax.ShapeDtypeStruct((share, count, cells), jnp.bfloat16)] * parts,
        scratch_shapes=[
            pltpu.VMEM((members, width, LANES), jnp.float32),
            pltpu.VMEM((slots, width, LANES), jnp.float32),
            pltpu.VMEM((width, LANES), jnp.float32),
        ],
        compiler_params=pltpu.CompilerParams(vmem_limit_bytes=32 * 1024 * 1024),
        cost_estimate=pl.CostEstimate(flops=10**9, bytes_accessed=50 * 10**6, transcendentals=0),
        interpret=INTERPRET,
    )(*states, dev, mix, keep)


def halo(cells, width):
    count = lax.axis_size("space")
    before = lax.ppermute(cells[-width:], "space", [(i, i + 1) for i in range(count - 1)])
    after = lax.ppermute(cells[:width], "space", [(i + 1, i) for i in range(count - 1)])
    return before, after


def wide_rows(cells, width):
    before, after = halo(cells, width)
    return jnp.concatenate([before, cells, after], axis=0)


def row_step(south, middle, north, courant):
    return (
        middle
        - 0.5 * courant * (north - south)
        + 0.5 * courant * courant * (north - 2.0 * middle + south)
    )


def col_step(middle, courant):
    padded = jnp.pad(middle, [(0, 0)] * (middle.ndim - 1) + [(1, 1)])
    east, west = padded[..., 2:], padded[..., :-2]
    return (
        middle
        - 0.5 * courant * (east - west)
        + 0.5 * courant * courant * (east - 2.0 * middle + west)
    )


def shards(
    ensemble, obs_value, obs_error, obs_cell, obs_species, patch_index, patch_count,
    courant_x, courant_y, dep_velocity, surface_factor,
):
    local_members, fields, tile_rows, columns = ensemble.shape
    species = dep_velocity.shape[0]
    levels = fields // species
    tile_cells = tile_rows * columns
    groups = lax.axis_size("mem")
    members = local_members * groups
    me = lax.axis_index("mem")
    slots = patch_index.shape[2]
    per_dev = tile_cells // groups
    paired = groups == 2 and tile_rows == 2 and columns == LANES and GROUP % levels == 0
    swap = [(0, 1), (1, 0)]

    if paired:
        tall = GROUP // levels
        small = jnp.concatenate(
            [
                obs_value,
                obs_error,
                (obs_cell // columns).astype(jnp.float32),
                (obs_cell % columns).astype(jnp.float32),
                (obs_species * (levels * tile_rows) + obs_cell // columns).astype(jnp.float32),
                jnp.zeros((GROUP - 5, obs_value.shape[1]), jnp.float32),
            ]
            + [courant_x.reshape(levels, tile_cells)] * tall
            + [courant_y.reshape(levels, tile_cells)] * tall,
            axis=0,
        )
        pool, edge, mine, theirs = prepare(
            ensemble.reshape(-1, columns), small, members, fields, tile_rows
        )
    else:
        surface = ensemble.reshape(local_members, species, levels, tile_cells)[:, :, 0]
        position = obs_species[0] * tile_cells + obs_cell[0]
        equiv = jnp.take(surface.reshape(local_members, -1), position, axis=1).astype(jnp.float32)
        equiv = lax.all_gather(equiv, "mem", axis=0, tiled=True)
        zeros = jnp.zeros_like(obs_value[0])
        info = jnp.stack(
            [
                obs_value[0],
                obs_error[0],
                (obs_cell[0] // columns).astype(jnp.float32),
                (obs_cell[0] % columns).astype(jnp.float32),
            ]
            + [zeros] * 4
        )
        packed = jnp.concatenate([equiv, info], axis=0)
        before, after = halo(packed[None], 1)
        offset = jnp.zeros((packed.shape[0], 1), jnp.float32).at[members + 2, 0].set(float(tile_rows))
        pool = jnp.concatenate([before[0] - offset, packed, after[0] + offset], axis=1)

    if paired:
        states = (mine, lax.ppermute(theirs, "mem", swap))
    else:
        states = (
            lax.all_to_all(
                ensemble.reshape(local_members, fields, tile_cells),
                "mem", split_axis=2, concat_axis=0, tiled=True,
            ),
        )
    spare = -per_dev % LANES
    pad = lambda a: jnp.pad(a, [(0, 0)] * (a.ndim - 1) + [(0, spare)]) if spare else a
    states = tuple(pad(state) for state in states)
    cell = me * per_dev + jnp.arange(per_dev, dtype=jnp.int32)
    dev, mix, keep = solve_cells(
        pool,
        pad(jnp.transpose(patch_index[0])),
        pad(patch_count),
        pad((cell // columns).astype(jnp.float32)[None]),
        pad((cell % columns).astype(jnp.float32)[None]),
        members,
    )

    width = next(w for w in (32, 16, fields) if fields % w == 0)
    blocks = fields // width
    parts = 2 if paired and blocks > 1 and width % levels == 0 else 1
    cuts = [0, (blocks + 1) // 2 * width, fields] if parts == 2 else [0, fields]
    if paired:
        tiled = edge.reshape(3, 2, GROUP, tile_rows, columns)[:, :, :levels]
        wide_x, wide_y = jnp.moveaxis(tiled, (1, 3), (0, 2)).reshape(2, 3 * tile_rows, levels, columns)
    else:
        wide_x = wide_rows(jnp.moveaxis(courant_x, 1, 0), SUBSTEPS)
        wide_y = wide_rows(jnp.moveaxis(courant_y, 1, 0), SUBSTEPS)
    loss = jnp.exp(-dep_velocity[:, None, None] * surface_factor[None])

    results = []
    for low, high in zip(cuts[:-1], cuts[1:]):
        count = high - low
        out = analyse(states, dev, mix, keep, slots, low, count, width)
        if paired:
            other = lax.ppermute(out[1], "mem", swap)
            rows = jnp.stack([jnp.where(me == 0, out[0], other), jnp.where(me == 0, other, out[0])])
        else:
            back = lax.all_to_all(out[0][..., :per_dev], "mem", split_axis=0, concat_axis=2, tiled=True)
            rows = jnp.moveaxis(back.reshape(local_members, count, tile_rows, columns), 2, 0)
        south, north = halo(rows, SUBSTEPS)
        shape = (local_members, count // levels, levels, columns)
        now = [
            part[r].reshape(shape).astype(jnp.float32)
            for part in (south, rows, north)
            for r in range(part.shape[0])
        ]
        for repeat in range(SUBSTEPS):
            first = repeat + 1
            now = [
                col_step(
                    row_step(now[r - 1], now[r], now[r + 1], wide_y[first + r - 1]),
                    wide_x[first + r - 1],
                )
                for r in range(1, len(now) - 1)
            ]
        part = loss[low // levels : high // levels]
        lowest = (jnp.arange(levels, dtype=jnp.int32) == 0)[:, None]
        now = [
            row * jnp.where(lowest, part[:, r][:, None], 1.0) for r, row in enumerate(now)
        ]
        joined = jnp.stack([row.astype(jnp.bfloat16) for row in now], axis=3)
        results.append(joined.reshape(local_members, count, tile_rows, columns))
    return jnp.concatenate(results, axis=1) if len(results) > 1 else results[0]


def solution(mesh):
    in_specs = (
        P("mem", None, "space", None),
        P("space", None),
        P("space", None),
        P("space", None),
        P("space", None),
        P("space", "mem", None),
        P("space", "mem"),
        P(None, "space", None),
        P(None, "space", None),
        P(),
        P("space", None),
    )
    out_specs = P("mem", None, "space", None)
    return jax.shard_map(shards, mesh=mesh, in_specs=in_specs, out_specs=out_specs, check_vma=False)
```

profile of v0, /device:TPU:17, one launch (start us, length us, event | category | flops | bytes accessed | tf_op | source)
XLA Modules:
  0.0 160.8 jit_solution(14722181523404030566)
XLA Ops:
  1.5 0.8 concatenate.8.small_ref
  2.3 1.7 %copy-done = bf16[32,160,2,128]{3,2,1,0:T(2,128)(2,1)S(1)} copy-done((bf16[32,160,2,128]{3,2,1,0:T(2,128)(2,1)S(1)}, bf16[32,160,2,128]{3,2,1,0:T(2,128)(2,1)}, u32[]{:S(2)}) %copy-start) | copy-done | bytes 2621464
  4.0 14.1 %shard_map.109 = (f32[72,768]{1,0:T(8,128)S(1)}, f32[3,16,256]{2,1,0:T(8,128)S(1)}, bf16[32,160,128]{2,1,0:T(8,128)(2,1)S(1)}, bf16[32,160,128]{2,1,0:T(8,128)(2,1)}) custom-call(bf16[10240,128]{1,0:T(8,128)(2,1)S(1)} %bitcast.135, f32[24,256]{1,0:T(8,128)S(1)} %concatenate.8.small_ref), custom_call_target="tpu_custom_call" | custom-call | flops 100000000 | bytes 8000000 | tf_op jit(solution)/shard_map/pallas_call | solution.py:350
  18.4 29.5 %shard_map.110 = (f32[2048,128]{1,0:T(8,128)S(1)}, f32[2048,128]{1,0:T(8,128)S(1)}, f32[1,128]{1,0:T(1,128)S(1)}) custom-call(f32[72,768]{1,0:T(8,128)S(1)} %get-tuple-element.18.pool_ref, s32[32,128]{1,0:T(8,128)S(1)} %bitcast.137, s32[1,128]{1,0:T(1,128)S(1)} %copy-done.2, f32[1,128]{1,0:T(1,128)S(1)} %get-tuple-element.89.row_ref, ...), custom_call_target="tpu_custom_call" | custom-call | flops 2000000000 | bytes 200000000 | tf_op jit(solution)/shard_map/pallas_call | solution.py:229
  48.0 1.0 collective-permute-done.refs_1_
  49.0 12.2 %shard_map.112 = (bf16[32,64,128]{2,1,0:T(8,128)(2,1)S(1)}, bf16[32,64,128]{2,1,0:T(8,128)(2,1)S(1)}) custom-call(bf16[32,160,128]{2,1,0:T(8,128)(2,1)S(1)} %get-tuple-element.16.refs_0_, bf16[32,160,128]{2,1,0:T(8,128)(2,1)S(1)} %collective-permute-done.refs_1_, f32[2048,128]{1,0:T(8,128)S(1)} %get-tuple-element.19.refs_2_, ...), custom_call_target="tpu_custom_call" | custom-call | flops 1000000000 | bytes 50000000 | tf_op jit(solution)/shard_map/pallas_call | solution.py:424
  61.7 18.3 %shard_map.111 = (bf16[32,96,128]{2,1,0:T(8,128)(2,1)S(1)}, bf16[32,96,128]{2,1,0:T(8,128)(2,1)S(1)}) custom-call(bf16[32,160,128]{2,1,0:T(8,128)(2,1)S(1)} %get-tuple-element.16.refs_0_, bf16[32,160,128]{2,1,0:T(8,128)(2,1)S(1)} %collective-permute-done.refs_1_, f32[2048,128]{1,0:T(8,128)S(1)} %get-tuple-element.19.refs_2_, ...), custom_call_target="tpu_custom_call" | custom-call | flops 1000000000 | bytes 50000000 | tf_op jit(solution)/shard_map/pallas_call | solution.py:424
  80.1 1.2 collective-permute-start.1
  81.6 2.9 %collective-permute-start.6 = (bf16[2,32,64,128]{3,2,1,0:T(8,128)(2,1)S(1)}, bf16[2,32,64,128]{3,2,1,0:T(8,128)(2,1)S(1)}, u32[]{:S(2)}, u32[]{:S(2)}) collective-permute-start(bf16[2,32,64,128]{3,2,1,0:T(8,128)(2,1)S(1)} %pad_maximum_fusion.1), channel_id=1, source_target_pairs={{1,0},{2,1},{3,2},{4,3},{5,4},{6,5},{7,6},{8,7},{9,8},{10,9},{11,1... | collective-permute-start | bytes 3145736 | tf_op jit(solution)/shard_map/ppermute | solution.py:446
  84.5 3.0 %collective-permute-start.5 = (bf16[2,32,64,128]{3,2,1,0:T(8,128)(2,1)S(1)}, bf16[2,32,64,128]{3,2,1,0:T(8,128)(2,1)S(1)}, u32[]{:S(2)}, u32[]{:S(2)}) collective-permute-start(bf16[2,32,64,128]{3,2,1,0:T(8,128)(2,1)S(1)} %pad_maximum_fusion.1), channel_id=1, source_target_pairs={{0,1},{1,2},{2,3},{3,4},{4,5},{5,6},{6,7},{7,8},{8,9},{9,10},{10,1... | collective-permute-start | bytes 3145736 | tf_op jit(solution)/shard_map/ppermute | solution.py:445
  87.6 10.9 %collective-permute-done.1 = bf16[32,96,128]{2,1,0:T(8,128)(2,1)S(1)} collective-permute-done((bf16[32,96,128]{2,1,0:T(8,128)(2,1)S(1)}, bf16[32,96,128]{2,1,0:T(8,128)(2,1)S(1)}, u32[]{:S(2)}, u32[]{:S(2)}) %collective-permute-start.1) | collective-permute-done | bytes 786464 | tf_op jit(solution)/shard_map/ppermute | solution.py:566
  99.0 3.5 %collective-permute-start.3 = (bf16[2,32,96,128]{3,2,1,0:T(8,128)(2,1)S(1)}, bf16[2,32,96,128]{3,2,1,0:T(8,128)(2,1)S(1)}, u32[]{:S(2)}, u32[]{:S(2)}) collective-permute-start(bf16[2,32,96,128]{3,2,1,0:T(8,128)(2,1)S(1)} %pad_maximum_fusion), channel_id=1, source_target_pairs={{1,0},{2,1},{3,2},{4,3},{5,4},{6,5},{7,6},{8,7},{9,8},{10,9},{11,1... | collective-permute-start | bytes 4718600 | tf_op jit(solution)/shard_map/ppermute | solution.py:446
  102.5 3.2 %collective-permute-start.2 = (bf16[2,32,96,128]{3,2,1,0:T(8,128)(2,1)S(1)}, bf16[2,32,96,128]{3,2,1,0:T(8,128)(2,1)S(1)}, u32[]{:S(2)}, u32[]{:S(2)}) collective-permute-start(bf16[2,32,96,128]{3,2,1,0:T(8,128)(2,1)S(1)} %pad_maximum_fusion), channel_id=1, source_target_pairs={{0,1},{1,2},{2,3},{3,4},{4,5},{5,6},{6,7},{7,8},{8,9},{9,10},{10,1... | collective-permute-start | bytes 4718600 | tf_op jit(solution)/shard_map/ppermute | solution.py:445
  105.7 20.5 %collective-permute-done.6 = bf16[2,32,64,128]{3,2,1,0:T(8,128)(2,1)S(1)} collective-permute-done((bf16[2,32,64,128]{3,2,1,0:T(8,128)(2,1)S(1)}, bf16[2,32,64,128]{3,2,1,0:T(8,128)(2,1)S(1)}, u32[]{:S(2)}, u32[]{:S(2)}) %collective-permute-start.6) | collective-permute-done | bytes 1048608 | tf_op jit(solution)/shard_map/ppermute | solution.py:446
  126.5 4.2 %multiply_add_fusion.9 = (f32[32,16,4,128]{3,0,2,1:T(8,128)S(1)}, f32[32,16,4,128]{3,0,2,1:T(8,128)S(1)}, f32[32,16,4,128]{3,0,2,1:T(8,128)S(1)}, f32[32,16,4,128]{3,0,2,1:T(8,128)S(1)}) fusion(f32[32,16,4,128]{3,2,1,0:T(4,128)S(1)} %bitcast.146, f32[32,16,4,128]{3,2,1,0:T(4,128)S(1)} %bitcast.147, f32[32,16,4,128]{3,2,1,0:T(4,128)S(1)} %bitcast.144, ...), kind=kLoop, calls=%fused_computation.39 | loop fusion | flops 8388608 | bytes 10502144 | tf_op jit(solution)/shard_map/add | solution.py:457
  130.7 1.7 %multiply_add_fusion.10 = (f32[32,16,4,128]{3,0,2,1:T(8,128)S(1)}, f32[32,16,4,128]{3,0,2,1:T(8,128)S(1)}, f32[32,16,4,128]{3,0,2,1:T(8,128)S(1)}) fusion(f32[32,16,4,128]{3,0,2,1:T(8,128)S(1)} %get-tuple-element.43, f32[4,128]{1,0:T(4,128)S(1)} %get-tuple-element.68, f32[4,128]{1,0:T(4,128)S(1)} %get-tuple-element.71, f32[4,128]{1,0:T(4,128)S(1)} %get-tuple-element.78, ...), kind=kLoop, calls=%fused_computation.41 | loop fusion | flops 8388608 | bytes 6307840 | tf_op jit(solution)/shard_map/add | solution.py:457
  132.4 1.1 multiply_add_fusion.8
  134.8 8.2 %collective-permute-done.3 = bf16[2,32,96,128]{3,2,1,0:T(8,128)(2,1)S(1)} collective-permute-done((bf16[2,32,96,128]{3,2,1,0:T(8,128)(2,1)S(1)}, bf16[2,32,96,128]{3,2,1,0:T(8,128)(2,1)S(1)}, u32[]{:S(2)}, u32[]{:S(2)}) %collective-permute-start.3) | collective-permute-done | bytes 1572896 | tf_op jit(solution)/shard_map/ppermute | solution.py:446
  143.7 6.6 %multiply_add_fusion.1 = (f32[32,24,4,128]{3,0,2,1:T(8,128)S(1)}, f32[32,24,4,128]{3,0,2,1:T(8,128)S(1)}, f32[32,24,4,128]{3,0,2,1:T(8,128)S(1)}, f32[32,24,4,128]{3,0,2,1:T(8,128)S(1)}) fusion(f32[32,24,4,128]{3,2,1,0:T(4,128)S(1)} %bitcast.140, f32[32,24,4,128]{3,2,1,0:T(4,128)S(1)} %bitcast.141, f32[32,24,4,128]{3,2,1,0:T(4,128)S(1)} %bitcast.138, ...), kind=kLoop, calls=%fused_computation.28 | loop fusion | flops 12582912 | bytes 15745024 | tf_op jit(solution)/shard_map/add | solution.py:457
  150.2 2.6 %multiply_add_fusion.2 = (f32[32,24,4,128]{3,0,2,1:T(8,128)S(1)}, f32[32,24,4,128]{3,0,2,1:T(8,128)S(1)}, f32[32,24,4,128]{3,0,2,1:T(8,128)S(1)}) fusion(f32[32,24,4,128]{3,0,2,1:T(8,128)S(1)} %get-tuple-element.39, f32[4,128]{1,0:T(4,128)S(1)} %get-tuple-element.68, f32[4,128]{1,0:T(4,128)S(1)} %get-tuple-element.71, f32[4,128]{1,0:T(4,128)S(1)} %get-tuple-element.78, ...), kind=kLoop, calls=%fused_computation.30 | loop fusion | flops 12582912 | bytes 9453568 | tf_op jit(solution)/shard_map/add | solution.py:457
  152.9 1.6 %multiply_add_fusion = f32[32,24,4,128]{3,0,2,1:T(8,128)S(1)} fusion(f32[32,24,4,128]{3,0,2,1:T(8,128)S(1)} %get-tuple-element.29, f32[32,24,4,128]{3,0,2,1:T(8,128)S(1)} %get-tuple-element.28, f32[32,24,4,128]{3,0,2,1:T(8,128)S(1)} %get-tuple-element.36, f32[4,128]{1,0:T(4,128)S(1)} %get-tuple-element.67, f32[4,128]{1,0:T(4,128)S(1)} %get-tuple-element.66, ...), kind=kLoop, calls=%fused_computation.27 | loop fusion | flops 6291456 | bytes 6299648 | tf_op jit(solution)/shard_map/add | solution.py:457
  154.5 0.9 multiply_convert_fusion
  155.4 0.9 multiply_convert_fusion.1
  156.6 4.2 %copy.60 = bf16[32,160,2,128]{3,2,1,0:T(2,128)(2,1)} copy(bf16[32,160,2,128]{3,0,1,2:T(8,128)(2,1)S(1)} %maximum_maximum_fusion) | data formatting | bytes 5242880 | tf_op jit(solution)/shard_map/concatenate | solution.py:594
  (42 shorter events, 5.7 us)
Async XLA Ops:
  0.0 18.4 %copy-start.4 = (f32[40]{0:T(128)S(1)}, f32[40]{0:T(128)}, u32[]{:S(2)}) copy-start(f32[40]{0:T(128)} %param.20) | copy-start | bytes 484
  0.0 18.4 %copy-start.1 = (s32[1,128,32]{1,2,0:T(8,128)S(1)}, s32[1,128,32]{1,2,0:T(8,128)}, u32[]{:S(2)}) copy-start(s32[1,128,32]{1,2,0:T(8,128)} %param.16) | copy-start | bytes 49156
  0.0 18.4 %copy-start.2 = (s32[1,128]{1,0:T(1,128)S(1)}, s32[1,128]{1,0:T(1,128)}, u32[]{:S(2)}) copy-start(s32[1,128]{1,0:T(1,128)} %cnt_ref.1) | copy-start | bytes 1540
  2.2 1.7 %copy-start = (bf16[32,160,2,128]{3,2,1,0:T(2,128)(2,1)S(1)}, bf16[32,160,2,128]{3,2,1,0:T(2,128)(2,1)}, u32[]{:S(2)}) copy-start(bf16[32,160,2,128]{3,2,1,0:T(2,128)(2,1)} %param.11) | copy-start | bytes 7864324
  18.1 30.9 %collective-permute-start = (bf16[32,160,128]{2,1,0:T(8,128)(2,1)}, bf16[32,160,128]{2,1,0:T(8,128)(2,1)S(1)}, u32[]{:S(2)}, u32[]{:S(2)}) collective-permute-start(bf16[32,160,128]{2,1,0:T(8,128)(2,1)} %get-tuple-element.17), channel_id=1, source_target_pairs={{0,16},{16,0},{1,17},{17,1},{2,18},{18,2},{3,19},{19,3},{4,20},{20... | collective-permute-start | bytes 3932168 | tf_op jit(solution)/shard_map/ppermute | solution.py:528
  18.4 29.5 %copy-start.3 = (f32[2,128]{1,0:T(2,128)S(1)}, f32[2,128]{1,0:T(2,128)}, u32[]{:S(2)}) copy-start(f32[2,128]{1,0:T(2,128)} %param.21) | copy-start | bytes 3076
  61.3 20.0 %collective-permute-start.4 = (bf16[32,64,128]{2,1,0:T(8,128)(2,1)S(1)}, bf16[32,64,128]{2,1,0:T(8,128)(2,1)S(1)}, u32[]{:S(2)}, u32[]{:S(2)}) collective-permute-start(bf16[32,64,128]{2,1,0:T(8,128)(2,1)S(1)} %get-tuple-element.26), channel_id=1, source_target_pairs={{0,16},{16,0},{1,17},{17,1},{2,18},{18,2},{3,19},{19,3},{4,20},{20... | collective-permute-start | bytes 1572872 | tf_op jit(solution)/shard_map/ppermute | solution.py:566
  80.1 18.4 %collective-permute-start.1 = (bf16[32,96,128]{2,1,0:T(8,128)(2,1)S(1)}, bf16[32,96,128]{2,1,0:T(8,128)(2,1)S(1)}, u32[]{:S(2)}, u32[]{:S(2)}) collective-permute-start(bf16[32,96,128]{2,1,0:T(8,128)(2,1)S(1)} %get-tuple-element.23), channel_id=1, source_target_pairs={{0,16},{16,0},{1,17},{17,1},{2,18},{18,2},{3,19},{19,3},{4,20},{20... | collective-permute-start | bytes 2359304 | tf_op jit(solution)/shard_map/ppermute | solution.py:566
  81.6 44.5 %collective-permute-start.6 = (bf16[2,32,64,128]{3,2,1,0:T(8,128)(2,1)S(1)}, bf16[2,32,64,128]{3,2,1,0:T(8,128)(2,1)S(1)}, u32[]{:S(2)}, u32[]{:S(2)}) collective-permute-start(bf16[2,32,64,128]{3,2,1,0:T(8,128)(2,1)S(1)} %pad_maximum_fusion.1), channel_id=1, source_target_pairs={{1,0},{2,1},{3,2},{4,3},{5,4},{6,5},{7,6},{8,7},{9,8},{10,9},{11,1... | collective-permute-start | bytes 3145736 | tf_op jit(solution)/shard_map/ppermute | solution.py:446
  84.5 41.8 %collective-permute-start.5 = (bf16[2,32,64,128]{3,2,1,0:T(8,128)(2,1)S(1)}, bf16[2,32,64,128]{3,2,1,0:T(8,128)(2,1)S(1)}, u32[]{:S(2)}, u32[]{:S(2)}) collective-permute-start(bf16[2,32,64,128]{3,2,1,0:T(8,128)(2,1)S(1)} %pad_maximum_fusion.1), channel_id=1, source_target_pairs={{0,1},{1,2},{2,3},{3,4},{4,5},{5,6},{6,7},{7,8},{8,9},{9,10},{10,1... | collective-permute-start | bytes 3145736 | tf_op jit(solution)/shard_map/ppermute | solution.py:445
  99.0 44.0 %collective-permute-start.3 = (bf16[2,32,96,128]{3,2,1,0:T(8,128)(2,1)S(1)}, bf16[2,32,96,128]{3,2,1,0:T(8,128)(2,1)S(1)}, u32[]{:S(2)}, u32[]{:S(2)}) collective-permute-start(bf16[2,32,96,128]{3,2,1,0:T(8,128)(2,1)S(1)} %pad_maximum_fusion), channel_id=1, source_target_pairs={{1,0},{2,1},{3,2},{4,3},{5,4},{6,5},{7,6},{8,7},{9,8},{10,9},{11,1... | collective-permute-start | bytes 4718600 | tf_op jit(solution)/shard_map/ppermute | solution.py:446
  102.5 40.8 %collective-permute-start.2 = (bf16[2,32,96,128]{3,2,1,0:T(8,128)(2,1)S(1)}, bf16[2,32,96,128]{3,2,1,0:T(8,128)(2,1)S(1)}, u32[]{:S(2)}, u32[]{:S(2)}) collective-permute-start(bf16[2,32,96,128]{3,2,1,0:T(8,128)(2,1)S(1)} %pad_maximum_fusion), channel_id=1, source_target_pairs={{0,1},{1,2},{2,3},{3,4},{4,5},{5,6},{6,7},{7,8},{8,9},{9,10},{10,1... | collective-permute-start | bytes 4718600 | tf_op jit(solution)/shard_map/ppermute | solution.py:445
where the time goes:
time: 162 us; the launch traced here: 161 us
  Pallas kernels  74.1 us (46%)
  waiting for transfers between devices  40.5 us (25%)
  other arithmetic  24 us (15%)
  starting transfers between devices  14.5 us (9%)
  local copies, waits for them, and re-layouts  7.43 us (5%)
    pallas_call x2, Pallas kernels, analyse(): pl.pallas_call(functools.partial(analysis_kernel, parts, slots), grid=(ce...  30.6 us
    pallas_call x1, Pallas kernels, solve_cells(): pl.pallas_call(functools.partial(weights_kernel, members, NEWTON, LOC), g...  29.5 us
    ppermute x2, waiting for transfers between devices, halo(): lax.ppermute(cells[:width], 'space', [(i + 1, i) for i in range(count - 1)])  28.7 us
    add x6, other arithmetic, row_step(): middle - 0.5 * courant * (north - south)  17.9 us
    pallas_call x1, Pallas kernels, prepare(): pl.pallas_call(functools.partial(prep_kernel, rows), in_specs=[vmem] * 2,...  14.1 us
    ppermute x2, waiting for transfers between devices, shards(): other = lax.ppermute(out[1], 'mem', swap)  10.9 us
    ppermute x2, starting transfers between devices, halo(): lax.ppermute(cells[:width], 'space', [(i + 1, i) for i in range(count - 1)])  6.37 us
    ppermute x2, starting transfers between devices, halo(): lax.ppermute(cells[-width:], 'space', [(i, i + 1) for i in range(count -...  6.23 us
  transfers between devices with their start and end apart: 7, of which 4 were waited for; matrix products, arithmetic and copies ran while one was open for 6% of the time, Pallas kernels for 30%

commit v1 on v0

--- a/solution.py
+++ b/solution.py
@@ -14,23 +14,25 @@
 LANES = 128
 GROUP = 8
 PITCH = 40
+WIDTH = 16
+LAG = 3
 INTERPRET = False
 
 
-def lane_product(left, right, depth, rows, width, finish, unroll=4):
-    def group(block, carry):
-        first = pl.multiple_of(block * GROUP, GROUP)
+def lane_product(left, right, depth, rows, width, finish, unroll=4, group=GROUP):
+    def several(block, carry):
+        first = pl.multiple_of(block * group, group)
 
         def step(k, sums):
             row = right(k)
-            return tuple(sums[r] + left(k, first, r) * row for r in range(GROUP))
+            return tuple(sums[r] + left(k, first, r) * row for r in range(group))
 
         zero = jnp.zeros((width, LANES), jnp.float32)
-        sums = lax.fori_loop(0, depth, step, (zero,) * GROUP, unroll=unroll)
+        sums = lax.fori_loop(0, depth, step, (zero,) * group, unroll=unroll)
         finish(first, sums)
         return carry
 
-    lax.fori_loop(0, rows // GROUP, group, 0)
+    lax.fori_loop(0, rows // group, several, 0)
 
 
 def weights_kernel(
@@ -416,6 +418,217 @@
         )
 
 
+def finish_kernel(
+    slots, width,
+    mine_ref, other_ref, dev_ref, mix_ref, keep_ref, edge_ref, loss_ref, out_ref,
+    rows, away, south, north, anomaly, mapped, mean_ref, coef, weave,
+    away_sent, away_come, edge_sent, edge_come,
+):
+    share, fields, _ = mine_ref.shape
+    members = 2 * share
+    chunks = fields // width
+    group = 2 * LANES // width
+    me, place, count = lax.axis_index("mem"), lax.axis_index("space"), lax.axis_size("space")
+    mesh_id = pl.DeviceIdType.MESH
+    exists = (place > 0, place + 1 < count)
+    sides = ((1 - me, place), (me, place - 1), (me, place + 1))
+    barrier = pltpu.get_barrier_semaphore()
+    pl.semaphore_signal(barrier, inc=1, device_id=sides[0], device_id_type=mesh_id)
+    for side in range(2):
+        @pl.when(exists[side])
+        def _():
+            pl.semaphore_signal(barrier, inc=1, device_id=sides[1 + side], device_id_type=mesh_id)
+
+    for side, buffer in enumerate((south, north)):
+        @pl.when(jnp.logical_not(exists[side]))
+        def _():
+            def clear(n, carry):
+                for r in range(2):
+                    buffer[r, n // share, n % share] = jnp.zeros((width, LANES), jnp.bfloat16)
+                return carry
+
+            lax.fori_loop(0, chunks * share, clear, 0)
+
+    lane = lax.broadcasted_iota(jnp.int32, (GROUP, LANES), 1)
+    for at, (part, r) in enumerate(((0, 1), (1, 0), (1, 1), (2, 0))):
+        cut = pl.ds(r * LANES, LANES)
+        cx = edge_ref[part, pl.ds(0, GROUP), cut]
+        cy = edge_ref[part, pl.ds(GROUP, GROUP), cut]
+        six = (
+            1.0 - cy * cy,
+            0.5 * cy * cy - 0.5 * cy,
+            0.5 * cy * cy + 0.5 * cy,
+            1.0 - cx * cx,
+            jnp.where(lane == LANES - 1, 0.0, 0.5 * cx * cx - 0.5 * cx),
+            jnp.where(lane == 0, 0.0, 0.5 * cx * cx + 0.5 * cx),
+        )
+        for n, value in enumerate(six):
+            for piece in range(width // GROUP):
+                coef[6 * at + n, pl.ds(piece * GROUP, GROUP), :] = value
+
+    greeted = 1 + exists[0].astype(jnp.int32) + exists[1].astype(jnp.int32)
+    pl.semaphore_wait(barrier, greeted)
+
+    def swap(q):
+        return pltpu.make_async_remote_copy(
+            src_ref=away.at[q], dst_ref=rows.at[me, q],
+            send_sem=away_sent.at[q], recv_sem=away_come.at[q],
+            device_id=sides[0], device_id_type=mesh_id,
+        )
+
+    def pass_on(side, r, q):
+        return pltpu.make_async_remote_copy(
+            src_ref=rows.at[r, q], dst_ref=(north, south)[side].at[r, q],
+            send_sem=edge_sent.at[side, r, q], recv_sem=edge_come.at[side, r, q],
+            device_id=sides[1 + side], device_id_type=mesh_id,
+        )
+
+    def pass_both(r, q):
+        for side in range(2):
+            @pl.when(exists[side])
+            def _():
+                pass_on(side, r, q).start()
+
+    def analyse_chunk(q):
+        cut = pl.ds(pl.multiple_of(q * width, width), width)
+        total = jnp.zeros((width, LANES), jnp.float32)
+        for state in (mine_ref, other_ref):
+            total = lax.fori_loop(
+                0, share, lambda i, t, s=state: t + s[i, cut, :].astype(jnp.float32), total, unroll=4
+            )
+        mean_ref[...] = total * (1.0 / members)
+        for part, state in enumerate((mine_ref, other_ref)):
+            def subtract(i, carry, s=state, base=part * share):
+                anomaly[base + i] = s[i, cut, :].astype(jnp.float32) - mean_ref[...]
+                return carry
+
+            lax.fori_loop(0, share, subtract, 0, unroll=4)
+
+        def to_mapped(first, sums):
+            for r in range(group):
+                mapped[first + r] = sums[r]
+
+        lane_product(
+            lambda i, first, r: dev_ref[pl.ds(i * slots + first + r, 1), :],
+            lambda i: anomaly[i], members, slots, width, to_mapped, group=group,
+        )
+        for part in (1, 0):
+            base = part * share
+
+            def to_out(first, sums, base=base, part=part):
+                for r in range(group):
+                    held = mean_ref[...] + keep_ref[...] * anomaly[base + first + r]
+                    value = (held + sums[r]).astype(jnp.bfloat16)
+                    if part:
+                        away[q, first + r] = value
+                    else:
+                        rows[me, q, first + r] = value
+
+            lane_product(
+                lambda k, first, r, base=base: mix_ref[pl.ds((base + first + r) * slots + k, 1), :],
+                lambda k: mapped[k], slots, share, width, to_out, group=group,
+            )
+            if part:
+                swap(q).start()
+            else:
+                pass_both(me, q)
+
+    def advect_chunk(q):
+        cut = pl.ds(pl.multiple_of(q * width, width), width)
+
+        def along(at, low, middle, high):
+            now = coef[6 * at] * middle + coef[6 * at + 1] * high + coef[6 * at + 2] * low
+            east = pltpu.roll(now, LANES - 1, 1)
+            west = pltpu.roll(now, 1, 1)
+            return coef[6 * at + 3] * now + coef[6 * at + 4] * east + coef[6 * at + 5] * west
+
+        def pair(n, carry):
+            for slot in range(2):
+                i = 2 * n + slot
+                now = [
+                    part[r, q, i].astype(jnp.float32) for part in (south, rows, north) for r in range(2)
+                ]
+                now = [along(at, *now[at : at + 3]) for at in range(4)]
+                now = [along(1 + at, *now[at : at + 3]) for at in range(2)]
+                for r in range(2):
+                    weave[slot, pl.ds(r, width, stride=2), :] = now[r] * loss_ref[r, cut, :]
+                start = pl.multiple_of((i * fields + q * width) * 2, 2 * width)
+                out_ref[pl.ds(start, 2 * width), :] = weave[slot].astype(jnp.bfloat16)
+            return carry
+
+        lax.fori_loop(0, share // 2, pair, 0)
+
+    def step(q, carry):
+        @pl.when(q < chunks)
+        def _():
+            analyse_chunk(q)
+
+        @pl.when((q >= 1) & (q - 1 < chunks))
+        def _():
+            swap(q - 1).wait_recv()
+            pass_both(1 - me, q - 1)
+
+        @pl.when((q >= LAG) & (q - LAG < chunks))
+        def _():
+            for side in range(2):
+                @pl.when(exists[1 - side])
+                def _():
+                    for r in range(2):
+                        pass_on(side, r, q - LAG).wait_recv()
+
+            advect_chunk(q - LAG)
+
+        return carry
+
+    lax.fori_loop(0, chunks + LAG, step, 0)
+
+    def drain(q, carry):
+        swap(q).wait_send()
+        for side in range(2):
+            @pl.when(exists[side])
+            def _():
+                for r in range(2):
+                    pass_on(side, r, q).wait_send()
+
+        return carry
+
+    lax.fori_loop(0, chunks, drain, 0)
+
+
+def finish(mine, other, dev, mix, keep, edge, loss, slots, rows):
+    share, fields, _ = mine.shape
+    width = WIDTH
+    chunks = fields // width
+    vmem = pl.BlockSpec(memory_space=pltpu.VMEM)
+    piece = (chunks, share, width, LANES)
+    return pl.pallas_call(
+        functools.partial(finish_kernel, slots, width),
+        in_specs=[vmem] * 7,
+        out_specs=vmem,
+        out_shape=jax.ShapeDtypeStruct((share * fields * rows, LANES), jnp.bfloat16),
+        scratch_shapes=[
+            pltpu.VMEM((2,) + piece, jnp.bfloat16),
+            pltpu.VMEM(piece, jnp.bfloat16),
+            pltpu.VMEM((2,) + piece, jnp.bfloat16),
+            pltpu.VMEM((2,) + piece, jnp.bfloat16),
+            pltpu.VMEM((2 * share, width, LANES), jnp.float32),
+            pltpu.VMEM((slots, width, LANES), jnp.float32),
+            pltpu.VMEM((width, LANES), jnp.float32),
+            pltpu.VMEM((24, width, LANES), jnp.float32),
+            pltpu.VMEM((2, 2 * width, LANES), jnp.float32),
+            pltpu.SemaphoreType.DMA((chunks,)),
+            pltpu.SemaphoreType.DMA((chunks,)),
+            pltpu.SemaphoreType.DMA((2, 2, chunks)),
+            pltpu.SemaphoreType.DMA((2, 2, chunks)),
+        ],
+        compiler_params=pltpu.CompilerParams(
+            vmem_limit_bytes=40 * 1024 * 1024, collective_id=1, has_side_effects=True
+        ),
+        cost_estimate=pl.CostEstimate(flops=10**9, bytes_accessed=10**7, transcendentals=0),
+        interpret=INTERPRET,
+    )(mine, other, dev, mix, keep, edge, loss)
+
+
 def analyse(states, dev, mix, keep, slots, first, count, width):
     share, _, cells = states[0].shape
     parts = len(states)
@@ -483,7 +696,8 @@
     me = lax.axis_index("mem")
     slots = patch_index.shape[2]
     per_dev = tile_cells // groups
-    paired = groups == 2 and tile_rows == 2 and columns == LANES and GROUP % levels == 0
+    paired = groups == 2 and tile_rows == 2 and columns == LANES
+    paired = paired and GROUP % levels == 0 and fields % WIDTH == 0
     swap = [(0, 1), (1, 0)]
 
     if paired:
@@ -546,52 +760,39 @@
         members,
     )
 
+    loss = jnp.exp(-dep_velocity[:, None, None] * surface_factor[None])
+    if paired:
+        lowest = (jnp.arange(levels, dtype=jnp.int32) == 0)[None, None, :, None]
+        factor = jnp.where(lowest, jnp.moveaxis(loss, 1, 0)[:, :, None], 1.0).reshape(tile_rows, fields, columns)
+        out = finish(*states, dev, mix, keep, edge, factor, slots, tile_rows)
+        return out.reshape(ensemble.shape)
+
     width = next(w for w in (32, 16, fields) if fields % w == 0)
-    blocks = fields // width
-    parts = 2 if paired and blocks > 1 and width % levels == 0 else 1
-    cuts = [0, (blocks + 1) // 2 * width, fields] if parts == 2 else [0, fields]
-    if paired:
-        tiled = edge.reshape(3, 2, GROUP, tile_rows, columns)[:, :, :levels]
-        wide_x, wide_y = jnp.moveaxis(tiled, (1, 3), (0, 2)).reshape(2, 3 * tile_rows, levels, columns)
-    else:
-        wide_x = wide_rows(jnp.moveaxis(courant_x, 1, 0), SUBSTEPS)
-        wide_y = wide_rows(jnp.moveaxis(courant_y, 1, 0), SUBSTEPS)
-    loss = jnp.exp(-dep_velocity[:, None, None] * surface_factor[None])
-
-    results = []
-    for low, high in zip(cuts[:-1], cuts[1:]):
-        count = high - low
-        out = analyse(states, dev, mix, keep, slots, low, count, width)
-        if paired:
-            other = lax.ppermute(out[1], "mem", swap)
-            rows = jnp.stack([jnp.where(me == 0, out[0], other), jnp.where(me == 0, other, out[0])])
-        else:
-            back = lax.all_to_all(out[0][..., :per_dev], "mem", split_axis=0, concat_axis=2, tiled=True)
-            rows = jnp.moveaxis(back.reshape(local_members, count, tile_rows, columns), 2, 0)
-        south, north = halo(rows, SUBSTEPS)
-        shape = (local_members, count // levels, levels, columns)
+    wide_x = wide_rows(jnp.moveaxis(courant_x, 1, 0), SUBSTEPS)
+    wide_y = wide_rows(jnp.moveaxis(courant_y, 1, 0), SUBSTEPS)
+    out = analyse(states, dev, mix, keep, slots, 0, fields, width)
+    back = lax.all_to_all(out[0][..., :per_dev], "mem", split_axis=0, concat_axis=2, tiled=True)
+    rows = jnp.moveaxis(back.reshape(local_members, fields, tile_rows, columns), 2, 0)
+    south, north = halo(rows, SUBSTEPS)
+    shape = (local_members, species, levels, columns)
+    now = [
+        part[r].reshape(shape).astype(jnp.float32)
+        for part in (south, rows, north)
+        for r in range(part.shape[0])
+    ]
+    for repeat in range(SUBSTEPS):
+        first = repeat + 1
         now = [
-            part[r].reshape(shape).astype(jnp.float32)
-            for part in (south, rows, north)
-            for r in range(part.shape[0])
+            col_step(
+                row_step(now[r - 1], now[r], now[r + 1], wide_y[first + r - 1]),
+                wide_x[first + r - 1],
+            )
+            for r in range(1, len(now) - 1)
         ]
-        for repeat in range(SUBSTEPS):
-            first = repeat + 1
-            now = [
-                col_step(
-                    row_step(now[r - 1], now[r], now[r + 1], wide_y[first + r - 1]),
-                    wide_x[first + r - 1],
-                )
-                for r in range(1, len(now) - 1)
-            ]
-        part = loss[low // levels : high // levels]
-        lowest = (jnp.arange(levels, dtype=jnp.int32) == 0)[:, None]
-        now = [
-            row * jnp.where(lowest, part[:, r][:, None], 1.0) for r, row in enumerate(now)
-        ]
-        joined = jnp.stack([row.astype(jnp.bfloat16) for row in now], axis=3)
-        results.append(joined.reshape(local_members, count, tile_rows, columns))
-    return jnp.concatenate(results, axis=1) if len(results) > 1 else results[0]
+    lowest = (jnp.arange(levels, dtype=jnp.int32) == 0)[:, None]
+    now = [row * jnp.where(lowest, loss[:, r][:, None], 1.0) for r, row in enumerate(now)]
+    joined = jnp.stack([row.astype(jnp.bfloat16) for row in now], axis=3)
+    return joined.reshape(local_members, fields, tile_rows, columns)
 
 
 def solution(mesh):

time: 162 us -> 126 us (0.78)
  Pallas kernels: 74.1 us -> 119 us
  waiting for transfers between devices: 40.5 us -> 0.73 us
  other arithmetic: 24 us -> 0.94 us
  starting transfers between devices: 14.5 us -> 0.29 us
  local copies, waits for them, and re-layouts: 7.43 us -> 4.87 us
    pallas_call x2 -> x1, Pallas kernels: 30.6 us -> 75.2 us  [finish(): pl.pallas_call(functools.partial(finish_kernel, slots, width), in_specs=[...]
    ppermute x6 -> x0, waiting for transfers between devices: 39.5 us -> none  [the longest x2 28.7 us: halo(): lax.ppermute(cells[:width], 'space', [(i + 1, i) for i in range(count - 1)])]
    add x6 -> x0, other arithmetic: 17.9 us -> none  [row_step(): middle - 0.5 * courant * (north - south)]
    ppermute x6 -> x0, starting transfers between devices: 14.2 us -> none  [the longest x2 6.37 us: halo(): lax.ppermute(cells[:width], 'space', [(i + 1, i) for i in range(count - 1)])]
    convert_element_type x10 -> x0, other arithmetic: 4.52 us -> none  [the longest x4 3.07 us: shards(): joined = jnp.stack([row.astype(jnp.bfloat16) for row in now], axis=3)]
    concatenate x1 -> x0, local copies, waits for them, and re-layouts: 4.19 us -> none  [shards(): return jnp.concatenate(results, axis=1) if len(results) > 1 else results[0]]
    unnamed x10 -> x11, local copies, waits for them, and re-layouts: 1.76 us -> 3.25 us
  transfers between devices with their start and end apart: 7 -> 1, of which waited for: 4 -> 1; matrix products, arithmetic and copies ran while one was open for 6% -> 0% of each run, Pallas kernels for 30% -> 23%
where the time goes in v1:
time: 126 us
  Pallas kernels  119 us (94%)
  local copies, waits for them, and re-layouts  4.87 us (4%)
    pallas_call x1, Pallas kernels, finish(): pl.pallas_call(functools.partial(finish_kernel, slots, width), in_specs=[...  75.2 us
    pallas_call x1, Pallas kernels, solve_cells(): pl.pallas_call(functools.partial(weights_kernel, members, NEWTON, LOC), g...  29.5 us
    pallas_call x1, Pallas kernels, prepare(): pl.pallas_call(functools.partial(prep_kernel, rows), in_specs=[vmem] * 2,...  14.1 us
    unnamed x11, local copies, waits for them, and re-layouts  3.25 us
  transfers between devices with their start and end apart: 1, of which 1 were waited for; matrix products, arithmetic and copies ran while one was open for 0% of the time, Pallas kernels for 23%

profile of v1, /device:TPU:17, one launch (start us, length us, event | category | flops | bytes accessed | tf_op | source)
XLA Modules:
  0.0 125.7 jit_solution(16471391382897413202)
XLA Ops:
  0.0 0.0 copy-start.4
  0.0 0.0 copy-start.2
  0.0 0.0 copy-start.1
  0.0 0.7 add_convert_fusion
  0.8 0.7 copy_bitcast_fusion
  1.5 0.8 concatenate.3.small_ref
  2.2 0.0 copy-start
  2.3 1.7 %copy-done = bf16[32,160,2,128]{3,2,1,0:T(2,128)(2,1)S(1)} copy-done((bf16[32,160,2,128]{3,2,1,0:T(2,128)(2,1)S(1)}, bf16[32,160,2,128]{3,2,1,0:T(2,128)(2,1)}, u32[]{:S(2)}) %copy-start) | copy-done | bytes 2621464
  4.0 14.1 %shard_map.109 = (f32[72,768]{1,0:T(8,128)S(1)}, f32[3,16,256]{2,1,0:T(8,128)S(1)}, bf16[32,160,128]{2,1,0:T(8,128)(2,1)S(1)}, bf16[32,160,128]{2,1,0:T(8,128)(2,1)}) custom-call(bf16[10240,128]{1,0:T(8,128)(2,1)S(1)} %bitcast.13, f32[24,256]{1,0:T(8,128)S(1)} %concatenate.3.small_ref), custom_call_target="tpu_custom_call" | custom-call | flops 100000000 | bytes 8000000 | tf_op jit(solution)/shard_map/pallas_call | solution.py:352
  18.1 0.3 collective-permute-start
  18.4 0.0 copy-done.4
  18.4 0.1 broadcast_in_dim.37
  18.6 0.0 copy-done.2
  18.6 0.0 copy-done.1
  18.6 0.0 copy-start.3
  18.6 29.5 %shard_map.110 = (f32[2048,128]{1,0:T(8,128)S(1)}, f32[2048,128]{1,0:T(8,128)S(1)}, f32[1,128]{1,0:T(1,128)S(1)}) custom-call(f32[72,768]{1,0:T(8,128)S(1)} %get-tuple-element.14.pool_ref, s32[32,128]{1,0:T(8,128)S(1)} %bitcast.14, s32[1,128]{1,0:T(1,128)S(1)} %copy-done.2, f32[1,128]{1,0:T(1,128)S(1)} %get-tuple-element.25.row_ref, ...), custom_call_target="tpu_custom_call" | custom-call | flops 2000000000 | bytes 200000000 | tf_op jit(solution)/shard_map/pallas_call | solution.py:231
  48.1 0.0 copy-done.3
  48.1 0.1 multiply_exponential_fusion
  48.2 0.1 broadcast_select_fusion.loss_ref
  48.3 0.7 collective-permute-done.other_ref
  49.0 75.2 %shard_map.111 = bf16[10240,128]{1,0:T(8,128)(2,1)S(1)} custom-call(bf16[32,160,128]{2,1,0:T(8,128)(2,1)S(1)} %get-tuple-element.12.mine_ref, bf16[32,160,128]{2,1,0:T(8,128)(2,1)S(1)} %collective-permute-done.other_ref, f32[2048,128]{1,0:T(8,128)S(1)} %get-tuple-element.15.dev_ref, f32[2048,128]{1,0:T(8,128)S(1)} %get-tuple-element.16.mix_ref, ...), custom_call_target="tpu_custom_call" | custom-call | flops 1000000000 | bytes 10000000 | tf_op jit(solution)/shard_map/pallas_call | solution.py:604
  124.2 1.5 %copy.17 = bf16[32,160,2,128]{3,2,1,0:T(2,128)(2,1)} copy(bf16[32,160,2,128]{3,2,1,0:T(2,128)(2,1)S(1)} %bitcast.12) | data formatting | bytes 5242880
  (8 shorter events, 0.1 us)
Async XLA Ops:
  0.0 18.4 %copy-start.4 = (f32[40]{0:T(128)S(1)}, f32[40]{0:T(128)}, u32[]{:S(2)}) copy-start(f32[40]{0:T(128)} %param.20) | copy-start | bytes 484
  0.0 18.6 %copy-start.2 = (s32[1,128]{1,0:T(1,128)S(1)}, s32[1,128]{1,0:T(1,128)}, u32[]{:S(2)}) copy-start(s32[1,128]{1,0:T(1,128)} %cnt_ref.1) | copy-start | bytes 1540
  0.0 18.6 %copy-start.1 = (s32[1,128,32]{1,2,0:T(8,128)S(1)}, s32[1,128,32]{1,2,0:T(8,128)}, u32[]{:S(2)}) copy-start(s32[1,128,32]{1,2,0:T(8,128)} %param.16) | copy-start | bytes 49156
  2.2 1.7 %copy-start = (bf16[32,160,2,128]{3,2,1,0:T(2,128)(2,1)S(1)}, bf16[32,160,2,128]{3,2,1,0:T(2,128)(2,1)}, u32[]{:S(2)}) copy-start(bf16[32,160,2,128]{3,2,1,0:T(2,128)(2,1)} %param.11) | copy-start | bytes 7864324
  18.1 30.9 %collective-permute-start = (bf16[32,160,128]{2,1,0:T(8,128)(2,1)}, bf16[32,160,128]{2,1,0:T(8,128)(2,1)S(1)}, u32[]{:S(2)}, u32[]{:S(2)}) collective-permute-start(bf16[32,160,128]{2,1,0:T(8,128)(2,1)} %get-tuple-element.13), channel_id=1, source_target_pairs={{0,16},{16,0},{1,17},{17,1},{2,18},{18,2},{3,19},{19,3},{4,20},{20... | collective-permute-start | bytes 3932168 | tf_op jit(solution)/shard_map/ppermute | solution.py:742
  18.6 29.5 %copy-start.3 = (f32[2,128]{1,0:T(2,128)S(1)}, f32[2,128]{1,0:T(2,128)}, u32[]{:S(2)}) copy-start(f32[2,128]{1,0:T(2,128)} %param.21) | copy-start | bytes 3076

commit v2 on v1

--- a/solution.py
+++ b/solution.py
@@ -16,6 +16,7 @@
 PITCH = 40
 WIDTH = 16
 LAG = 3
+UNROLL = 4
 INTERPRET = False
 
 
@@ -542,9 +543,9 @@
             west = pltpu.roll(now, 1, 1)
             return coef[6 * at + 3] * now + coef[6 * at + 4] * east + coef[6 * at + 5] * west
 
-        def pair(n, carry):
-            for slot in range(2):
-                i = 2 * n + slot
+        def several(n, carry):
+            for slot in range(UNROLL):
+                i = UNROLL * n + slot
                 now = [
                     part[r, q, i].astype(jnp.float32) for part in (south, rows, north) for r in range(2)
                 ]
@@ -556,7 +557,7 @@
                 out_ref[pl.ds(start, 2 * width), :] = weave[slot].astype(jnp.bfloat16)
             return carry
 
-        lax.fori_loop(0, share // 2, pair, 0)
+        lax.fori_loop(0, share // UNROLL, several, 0)
 
     def step(q, carry):
         @pl.when(q < chunks)
@@ -615,7 +616,7 @@
             pltpu.VMEM((slots, width, LANES), jnp.float32),
             pltpu.VMEM((width, LANES), jnp.float32),
             pltpu.VMEM((24, width, LANES), jnp.float32),
-            pltpu.VMEM((2, 2 * width, LANES), jnp.float32),
+            pltpu.VMEM((UNROLL, 2 * width, LANES), jnp.float32),
             pltpu.SemaphoreType.DMA((chunks,)),
             pltpu.SemaphoreType.DMA((chunks,)),
             pltpu.SemaphoreType.DMA((2, 2, chunks)),

time: 126 us -> 119 us (0.944)
  Pallas kernels: 119 us -> 112 us
    pallas_call x1, Pallas kernels: 75.2 us -> 68.1 us  [finish(): pl.pallas_call(functools.partial(finish_kernel, slots, width), in_specs=[...]
  transfers between devices with their start and end apart: 1 -> 1, of which waited for: 1 -> 1; matrix products, arithmetic and copies ran while one was open for 0% -> 0% of each run, Pallas kernels for 23% -> 25%
where the time goes in v2:
time: 119 us
  Pallas kernels  112 us (94%)
  local copies, waits for them, and re-layouts  4.87 us (4%)
    pallas_call x1, Pallas kernels, finish(): pl.pallas_call(functools.partial(finish_kernel, slots, width), in_specs=[...  68.1 us
    pallas_call x1, Pallas kernels, solve_cells(): pl.pallas_call(functools.partial(weights_kernel, members, NEWTON, LOC), g...  29.5 us
    pallas_call x1, Pallas kernels, prepare(): pl.pallas_call(functools.partial(prep_kernel, rows), in_specs=[vmem] * 2,...  14.1 us
    unnamed x11, local copies, waits for them, and re-layouts  3.25 us
  transfers between devices with their start and end apart: 1, of which 1 were waited for; matrix products, arithmetic and copies ran while one was open for 0% of the time, Pallas kernels for 25%

profile of v2, /device:TPU:17, one launch (start us, length us, event | category | flops | bytes accessed | tf_op | source)
XLA Modules:
  0.0 118.7 jit_solution(368219072421525972)
XLA Ops:
  0.0 0.0 copy-start.4
  0.0 0.0 copy-start.2
  0.0 0.0 copy-start.1
  0.0 0.7 add_convert_fusion
  0.8 0.7 copy_bitcast_fusion
  1.5 0.8 concatenate.3.small_ref
  2.2 0.0 copy-start
  2.3 1.7 %copy-done = bf16[32,160,2,128]{3,2,1,0:T(2,128)(2,1)S(1)} copy-done((bf16[32,160,2,128]{3,2,1,0:T(2,128)(2,1)S(1)}, bf16[32,160,2,128]{3,2,1,0:T(2,128)(2,1)}, u32[]{:S(2)}) %copy-start) | copy-done | bytes 2621464
  4.0 14.1 %shard_map.109 = (f32[72,768]{1,0:T(8,128)S(1)}, f32[3,16,256]{2,1,0:T(8,128)S(1)}, bf16[32,160,128]{2,1,0:T(8,128)(2,1)S(1)}, bf16[32,160,128]{2,1,0:T(8,128)(2,1)}) custom-call(bf16[10240,128]{1,0:T(8,128)(2,1)S(1)} %bitcast.13, f32[24,256]{1,0:T(8,128)S(1)} %concatenate.3.small_ref), custom_call_target="tpu_custom_call" | custom-call | flops 100000000 | bytes 8000000 | tf_op jit(solution)/shard_map/pallas_call | solution.py:353
  18.1 0.3 collective-permute-start
  18.4 0.0 copy-done.4
  18.4 0.1 broadcast_in_dim.37
  18.6 0.0 copy-done.2
  18.6 0.0 copy-done.1
  18.6 0.0 copy-start.3
  18.6 29.5 %shard_map.110 = (f32[2048,128]{1,0:T(8,128)S(1)}, f32[2048,128]{1,0:T(8,128)S(1)}, f32[1,128]{1,0:T(1,128)S(1)}) custom-call(f32[72,768]{1,0:T(8,128)S(1)} %get-tuple-element.14.pool_ref, s32[32,128]{1,0:T(8,128)S(1)} %bitcast.14, s32[1,128]{1,0:T(1,128)S(1)} %copy-done.2, f32[1,128]{1,0:T(1,128)S(1)} %get-tuple-element.25.row_ref, ...), custom_call_target="tpu_custom_call" | custom-call | flops 2000000000 | bytes 200000000 | tf_op jit(solution)/shard_map/pallas_call | solution.py:232
  48.1 0.0 copy-done.3
  48.1 0.1 multiply_exponential_fusion
  48.2 0.1 broadcast_select_fusion.loss_ref
  48.3 0.7 collective-permute-done.other_ref
  49.0 68.1 %shard_map.111 = bf16[10240,128]{1,0:T(8,128)(2,1)S(1)} custom-call(bf16[32,160,128]{2,1,0:T(8,128)(2,1)S(1)} %get-tuple-element.12.mine_ref, bf16[32,160,128]{2,1,0:T(8,128)(2,1)S(1)} %collective-permute-done.other_ref, f32[2048,128]{1,0:T(8,128)S(1)} %get-tuple-element.15.dev_ref, f32[2048,128]{1,0:T(8,128)S(1)} %get-tuple-element.16.mix_ref, ...), custom_call_target="tpu_custom_call" | custom-call | flops 1000000000 | bytes 10000000 | tf_op jit(solution)/shard_map/pallas_call | solution.py:605
  117.2 1.5 %copy.17 = bf16[32,160,2,128]{3,2,1,0:T(2,128)(2,1)} copy(bf16[32,160,2,128]{3,2,1,0:T(2,128)(2,1)S(1)} %bitcast.12) | data formatting | bytes 5242880
  (8 shorter events, 0.1 us)
Async XLA Ops:
  0.0 18.4 %copy-start.4 = (f32[40]{0:T(128)S(1)}, f32[40]{0:T(128)}, u32[]{:S(2)}) copy-start(f32[40]{0:T(128)} %param.20) | copy-start | bytes 484
  0.0 18.6 %copy-start.2 = (s32[1,128]{1,0:T(1,128)S(1)}, s32[1,128]{1,0:T(1,128)}, u32[]{:S(2)}) copy-start(s32[1,128]{1,0:T(1,128)} %cnt_ref.1) | copy-start | bytes 1540
  0.0 18.6 %copy-start.1 = (s32[1,128,32]{1,2,0:T(8,128)S(1)}, s32[1,128,32]{1,2,0:T(8,128)}, u32[]{:S(2)}) copy-start(s32[1,128,32]{1,2,0:T(8,128)} %param.16) | copy-start | bytes 49156
  2.2 1.7 %copy-start = (bf16[32,160,2,128]{3,2,1,0:T(2,128)(2,1)S(1)}, bf16[32,160,2,128]{3,2,1,0:T(2,128)(2,1)}, u32[]{:S(2)}) copy-start(bf16[32,160,2,128]{3,2,1,0:T(2,128)(2,1)} %param.11) | copy-start | bytes 7864324
  18.1 30.9 %collective-permute-start = (bf16[32,160,128]{2,1,0:T(8,128)(2,1)}, bf16[32,160,128]{2,1,0:T(8,128)(2,1)S(1)}, u32[]{:S(2)}, u32[]{:S(2)}) collective-permute-start(bf16[32,160,128]{2,1,0:T(8,128)(2,1)} %get-tuple-element.13), channel_id=1, source_target_pairs={{0,16},{16,0},{1,17},{17,1},{2,18},{18,2},{3,19},{19,3},{4,20},{20... | collective-permute-start | bytes 3932168 | tf_op jit(solution)/shard_map/ppermute | solution.py:743
  18.6 29.5 %copy-start.3 = (f32[2,128]{1,0:T(2,128)S(1)}, f32[2,128]{1,0:T(2,128)}, u32[]{:S(2)}) copy-start(f32[2,128]{1,0:T(2,128)} %param.21) | copy-start | bytes 3076

commit v3 on v2

--- a/solution.py
+++ b/solution.py
@@ -40,7 +40,7 @@
     members, repeats, radius,
     pool_ref, idx_ref, cnt_ref, row_ref, col_ref,
     dev_ref, mix_ref, keep_ref,
-    first_v, now_v, step_g, keys, tail, innov, scal,
+    first_v, one_v, two_v, step_g, keys, innov, scal,
 ):
     slots = idx_ref.shape[0]
     pooled = pool_ref.shape[1]
@@ -69,11 +69,11 @@
         rho = jnp.exp(-dist / (2.0 * radius * radius)) / facts[1:2]
         scale = jnp.sqrt(jnp.where(k < cnt_ref[...], rho, 0.0))
         scaled = (equiv - mean) * scale
-        dev_ref[pl.ds(k, members, stride=slots), :] = scaled
+        dev_ref[pl.ds(k, members, stride=PITCH), :] = scaled
         innov[pl.ds(k, 1), :] = (facts[0:1] - mean) * scale
         return total + jnp.sum(scaled * scaled, axis=0, keepdims=True)
 
-    spread = lax.fori_loop(0, slots, pick, jnp.zeros((1, LANES), jnp.float32), unroll=2)
+    spread = lax.fori_loop(0, slots, pick, jnp.zeros((1, LANES), jnp.float32), unroll=8)
     shift = members - 1.0
     inverse = 1.0 / (spread + shift * members)
     level = lax.broadcasted_iota(jnp.int32, (GROUP, LANES), 0)
@@ -92,7 +92,7 @@
             if j < i // GROUP:
                 ref[pl.ds(base + j * GROUP * PITCH + i, GROUP, stride=PITCH), :] = part
 
-    def product(left, right, depth, finish, unroll=4):
+    def product(left, right, depth, finish, unroll=16):
         for pair in range((blocks + 1) // 2):
             groups = sorted({pair, blocks - 1 - pair})
 
@@ -116,21 +116,19 @@
                     finish(g * GROUP + r, sums[spot : spot + g + 1])
                     spot += g + 1
 
-    def square(left, right, finish, left_base=0):
+    def square(left, right, finish, base=0):
         product(
-            lambda k, i: left[pl.ds(left_base + k * PITCH + i, 1), :],
+            lambda k, i: left[pl.ds(base + k * PITCH + i, 1), :],
             lambda k, j: at(right, k, j),
             slots, finish,
         )
 
     def gram_done(i, sums):
-        parts = [part * inverse for part in sums]
-        put(first_v, i, parts)
-        put(now_v, i, parts)
+        put(first_v, i, [part * inverse for part in sums])
 
     product(
-        lambda k, i: dev_ref[pl.ds(k * slots + i, 1), :],
-        lambda k, j: dev_ref[pl.ds(pl.multiple_of(k * slots, slots) + j * GROUP, GROUP), :],
+        lambda k, i: dev_ref[pl.ds(k * PITCH + i, 1), :],
+        lambda k, j: at(dev_ref, k, j),
         members, gram_done,
     )
 
@@ -149,51 +147,57 @@
     last_z = after
     area = slots * PITCH
 
-    def forward(n, carry):
+    def forward(n, old, new):
         xi = scal[pl.ds(n, 1), :]
         mu = scal[pl.ds(repeats + n, 1), :]
         flat, slope = mu * mu - xi * mu, 0.25 * xi - mu
         base = pl.multiple_of(n * area, GROUP)
 
         def to_g(i, sums):
-            parts = [0.25 * part + slope * at(now_v, i, j) for j, part in enumerate(sums)]
+            parts = [0.25 * part + slope * at(old, i, j) for j, part in enumerate(sums)]
             parts[-1] = parts[-1] + eye(i % GROUP, flat)
             put(step_g, i, parts)
 
-        square(now_v, now_v, to_g)
+        square(old, old, to_g)
 
         def to_v(i, sums):
-            put(tail, i, sums)
+            put(new, i, sums)
             put(keys, i, [mu * at(step_g, i, j) - 0.5 * part for j, part in enumerate(sums)], base)
 
-        square(step_g, now_v, to_v)
-        now_v[...] = tail[...]
+        square(step_g, old, to_v)
+
+    def forward_pair(n, carry):
+        forward(2 * n + 1, one_v, two_v)
+        forward(2 * n + 2, two_v, one_v)
         return carry
 
-    lax.fori_loop(0, repeats - 1, forward, 0)
+    forward(0, first_v, one_v)
+    lax.fori_loop(0, repeats // 2 - 1, forward_pair, 0)
 
     after = scal[pl.ds(3 * repeats - 2, 1), :]
     for i in range(slots):
         parts = [-0.5 * at(keys, i, j, (repeats - 2) * area) for j in range(blocks)]
         parts[i // GROUP] = parts[i // GROUP] - eye(i % GROUP, 0.5 * after)
         for j, part in enumerate(parts):
-            now_v[pl.ds(i * PITCH + j * GROUP, GROUP), :] = part
-
-    def backward(m, carry):
-        n = repeats - 3 - m
+            one_v[pl.ds(i * PITCH + j * GROUP, GROUP), :] = part
+
+    def backward(n, old, new):
         base = pl.multiple_of(n * area, GROUP)
         half = 0.5 * scal[pl.ds(2 * repeats + n, 1), :]
 
         def to_h(i, sums):
             parts = list(sums)
             parts[-1] = parts[-1] - eye(i % GROUP, half)
-            put(tail, i, parts)
-
-        square(keys, now_v, to_h, base)
-        now_v[...] = tail[...]
+            put(new, i, parts)
+
+        square(keys, old, to_h, base)
+
+    def backward_pair(m, carry):
+        backward(repeats - 3 - 2 * m, one_v, two_v)
+        backward(repeats - 4 - 2 * m, two_v, one_v)
         return carry
 
-    lax.fori_loop(0, repeats - 2, backward, 0)
+    lax.fori_loop(0, repeats // 2 - 1, backward_pair, 0)
 
     def whole(ref, k):
         return ref[pl.ds(pl.multiple_of(k * PITCH, GROUP), slots), :]
@@ -208,7 +212,7 @@
 
     for _ in range(2):
         start = innov[...]
-        innov[...] = apply(now_v)
+        innov[...] = apply(one_v)
         innov[...] = last_z * start + apply(first_v)
     gain = innov[...] * inverse
     factor = math.sqrt(shift) * jnp.sqrt(inverse)
@@ -220,8 +224,8 @@
             mix_ref[pl.ds(pl.multiple_of((first + r) * slots, slots), slots), :] = both * sums[r] + gain
 
     lane_product(
-        lambda k, first, r: dev_ref[pl.ds((first + r) * slots + k, 1), :],
-        lambda k: whole(now_v, k), slots, members, slots, to_mix,
+        lambda k, first, r: dev_ref[pl.ds((first + r) * PITCH + k, 1), :],
+        lambda k: whole(one_v, k), slots, members, slots, to_mix, unroll=16,
     )
 
 
@@ -233,15 +237,18 @@
         functools.partial(weights_kernel, members, NEWTON, LOC),
         grid=(cells // LANES,),
         in_specs=[pl.BlockSpec(pool.shape, lambda c: (0, 0)), lane(slots), lane(1), lane(1), lane(1)],
-        out_specs=[lane(members * slots), lane(members * slots), lane(1)],
+        out_specs=[lane(members * PITCH), lane(members * slots), lane(1)],
         out_shape=[
-            jax.ShapeDtypeStruct((members * slots, cells), jnp.float32),
+            jax.ShapeDtypeStruct((members * PITCH, cells), jnp.float32),
             jax.ShapeDtypeStruct((members * slots, cells), jnp.float32),
             jax.ShapeDtypeStruct((1, cells), jnp.float32),
         ],
-        scratch_shapes=[square] * 3 + [
+        scratch_shapes=[
+            square,
+            square,
+            square,
+            square,
             pltpu.VMEM(((NEWTON - 1) * slots * PITCH, LANES), jnp.float32),
-            square,
             pltpu.VMEM((slots, LANES), jnp.float32),
             pltpu.VMEM((3 * NEWTON, LANES), jnp.float32),
         ],
@@ -251,11 +258,12 @@
     )(pool, idx, counts, rows, cols)
 
 
-def prep_kernel(rows, ens_ref, small_ref, pool_ref, edge_ref, mine_ref, theirs_ref, block, land, spread, send_sems, recv_sems):
+def prep_kernel(rows, levels, ens_ref, small_ref, pool_ref, edge_ref, mine_ref, theirs_ref, block, land, spread, send_sems, recv_sems):
     share, fields, _ = mine_ref.shape
     observed = small_ref.shape[1]
     span = fields * rows
     facts = small_ref.shape[0]
+    species = fields // levels
     me, place, count = lax.axis_index("mem"), lax.axis_index("space"), lax.axis_size("space")
 
     def exists(step):
@@ -283,16 +291,20 @@
     hot = jnp.where(
         lax.broadcasted_iota(jnp.int32, (LANES, observed), 0).astype(jnp.float32) == small_ref[3:4, :], 1.0, 0.0
     ).astype(jnp.bfloat16)
-    wanted = lax.broadcasted_iota(jnp.int32, (span, observed), 0).astype(jnp.float32) == small_ref[4:5, :]
-
-    def look(i, carry):
-        got = jnp.dot(
-            ens_ref[pl.ds(pl.multiple_of(i * span, span), span), :], hot, preferred_element_type=jnp.float32
-        )
-        block[pl.ds(i, 1), :] = jnp.sum(jnp.where(wanted, got, 0.0), axis=0, keepdims=True)
+    wanted = lax.broadcasted_iota(jnp.int32, (rows * species, observed), 0).astype(jnp.float32) == small_ref[4:5, :]
+
+    def look(n, carry):
+        for slot in range(UNROLL):
+            i = UNROLL * n + slot
+            spread[slot] = ens_ref[pl.ds(pl.multiple_of(i * span, span), span), :].astype(jnp.float32)
+            lowest = jnp.concatenate(
+                [spread[slot, pl.ds(r, species, stride=rows * levels), :] for r in range(rows)], axis=0
+            )
+            got = jnp.dot(lowest.astype(jnp.bfloat16), hot, preferred_element_type=jnp.float32)
+            block[pl.ds(i, 1), :] = jnp.sum(jnp.where(wanted, got, 0.0), axis=0, keepdims=True)
         return carry
 
-    lax.fori_loop(0, share, look, 0)
+    lax.fori_loop(0, share // UNROLL, look, 0)
 
     greeted = 1 + 2 * exists(-1).astype(jnp.int32) + 2 * exists(1).astype(jnp.int32)
     pl.semaphore_wait(barrier, greeted)
@@ -308,15 +320,15 @@
     for n, (flip, step) in enumerate(ways):
         guard(step, lambda n=n: copy(n).start())
 
-    def split(pair, carry):
-        for slot in range(2):
-            i = 2 * pair + slot
+    def split(n, carry):
+        for slot in range(UNROLL):
+            i = UNROLL * n + slot
             spread[slot] = ens_ref[pl.ds(pl.multiple_of(i * span, span), span), :].astype(jnp.float32)
             mine_ref[i] = spread[slot, pl.ds(me, fields, stride=rows), :].astype(jnp.bfloat16)
             theirs_ref[i] = spread[slot, pl.ds(1 - me, fields, stride=rows), :].astype(jnp.bfloat16)
         return carry
 
-    lax.fori_loop(0, share // 2, split, 0)
+    lax.fori_loop(0, share // UNROLL, split, 0)
 
     for n, (flip, step) in enumerate(ways):
         def arrive(n=n):
@@ -345,13 +357,13 @@
         edge_ref[part] = own[share + GROUP :]
 
 
-def prepare(flat, small, members, fields, rows):
+def prepare(flat, small, members, fields, rows, levels):
     share = members // 2
     observed = small.shape[1]
     high = share + small.shape[0]
     vmem = pl.BlockSpec(memory_space=pltpu.VMEM)
     return pl.pallas_call(
-        functools.partial(prep_kernel, rows),
+        functools.partial(prep_kernel, rows, levels),
         in_specs=[vmem] * 2,
         out_specs=[vmem] * 4,
         out_shape=[
@@ -363,7 +375,7 @@
         scratch_shapes=[
             pltpu.VMEM((high, observed), jnp.float32),
             pltpu.VMEM((3, 2, high, observed), jnp.float32),
-            pltpu.VMEM((2, fields * rows, LANES), jnp.float32),
+            pltpu.VMEM((UNROLL, fields * rows, LANES), jnp.float32),
             pltpu.SemaphoreType.DMA((5,)),
             pltpu.SemaphoreType.DMA((3, 2)),
         ],
@@ -402,7 +414,7 @@
             mapped[first + r] = sums[r]
 
     lane_product(
-        lambda i, first, r: dev_ref[pl.ds(i * slots + first + r, 1), :],
+        lambda i, first, r: dev_ref[pl.ds(i * PITCH + first + r, 1), :],
         lambda i: anomaly[i], members, slots, width, to_mapped,
     )
     for part, out in enumerate(outs):
@@ -510,7 +522,7 @@
                 mapped[first + r] = sums[r]
 
         lane_product(
-            lambda i, first, r: dev_ref[pl.ds(i * slots + first + r, 1), :],
+            lambda i, first, r: dev_ref[pl.ds(i * PITCH + first + r, 1), :],
             lambda i: anomaly[i], members, slots, width, to_mapped, group=group,
         )
         for part in (1, 0):
@@ -640,7 +652,7 @@
         grid=(cells // LANES, count // width),
         in_specs=[
             pl.BlockSpec((share, width, LANES), lambda c, f: (0, f + first // width, c))
-        ] * parts + [wide(members * slots), wide(members * slots), wide(1)],
+        ] * parts + [wide(members * PITCH), wide(members * slots), wide(1)],
         out_specs=[pl.BlockSpec((share, width, LANES), lambda c, f: (0, f, c))] * parts,
         out_shape=[jax.ShapeDtypeStruct((share, count, cells), jnp.bfloat16)] * parts,
         scratch_shapes=[
@@ -698,7 +710,8 @@
     slots = patch_index.shape[2]
     per_dev = tile_cells // groups
     paired = groups == 2 and tile_rows == 2 and columns == LANES
-    paired = paired and GROUP % levels == 0 and fields % WIDTH == 0
+    paired = paired and GROUP % levels == 0 and fields % WIDTH == 0 and species % GROUP == 0
+    paired = paired and local_members % UNROLL == 0
     swap = [(0, 1), (1, 0)]
 
     if paired:
@@ -709,7 +722,7 @@
                 obs_error,
                 (obs_cell // columns).astype(jnp.float32),
                 (obs_cell % columns).astype(jnp.float32),
-                (obs_species * (levels * tile_rows) + obs_cell // columns).astype(jnp.float32),
+                (obs_cell // columns * species + obs_species).astype(jnp.float32),
                 jnp.zeros((GROUP - 5, obs_value.shape[1]), jnp.float32),
             ]
             + [courant_x.reshape(levels, tile_cells)] * tall
@@ -717,7 +730,7 @@
             axis=0,
         )
         pool, edge, mine, theirs = prepare(
-            ensemble.reshape(-1, columns), small, members, fields, tile_rows
+            ensemble.reshape(-1, columns), small, members, fields, tile_rows, levels
         )
     else:
         surface = ensemble.reshape(local_members, species, levels, tile_cells)[:, :, 0]

time: 119 us -> 114 us (0.958)
  Pallas kernels: 112 us -> 101 us
  waiting for transfers between devices: 0.73 us -> 5.58 us
    pallas_call x1, Pallas kernels: 29.5 us -> 23.2 us  [solve_cells(): pl.pallas_call(functools.partial(weights_kernel, members, NEWTON, LOC), g...]
    pallas_call x1, Pallas kernels: 14.1 us -> 8.84 us  [prepare(): pl.pallas_call(functools.partial(prep_kernel, rows, levels), in_specs=[vm...]
    ppermute x1, waiting for transfers between devices: 0.73 us -> 5.58 us  [shards(): states = (mine, lax.ppermute(theirs, 'mem', swap))]
  transfers between devices with their start and end apart: 1 -> 1, of which waited for: 1 -> 1; matrix products, arithmetic and copies ran while one was open for 0% -> 0% of each run, Pallas kernels for 25% -> 20%
where the time goes in v3:
time: 114 us
  Pallas kernels  101 us (89%)
  waiting for transfers between devices  5.58 us (5%)
  local copies, waits for them, and re-layouts  4.87 us (4%)
  starting transfers between devices  1.37 us (1%)
    pallas_call x1, Pallas kernels, finish(): pl.pallas_call(functools.partial(finish_kernel, slots, width), in_specs=[...  69 us
    pallas_call x1, Pallas kernels, solve_cells(): pl.pallas_call(functools.partial(weights_kernel, members, NEWTON, LOC), g...  23.2 us
    pallas_call x1, Pallas kernels, prepare(): pl.pallas_call(functools.partial(prep_kernel, rows, levels), in_specs=[vm...  8.84 us
    ppermute x1, waiting for transfers between devices, shards(): states = (mine, lax.ppermute(theirs, 'mem', swap))  5.58 us
    unnamed x11, local copies, waits for them, and re-layouts  3.25 us
  transfers between devices with their start and end apart: 1, of which 1 were waited for; matrix products, arithmetic and copies ran while one was open for 0% of the time, Pallas kernels for 20%

profile of v3, /device:TPU:17, one launch (start us, length us, event | category | flops | bytes accessed | tf_op | source)
XLA Modules:
  0.0 113.9 jit_solution(2710436867952515829)
XLA Ops:
  0.0 0.7 add_convert_fusion
  0.7 0.7 copy_bitcast_fusion
  1.4 0.8 concatenate.3.small_ref
  2.2 0.0 copy-start
  2.2 1.7 %copy-done = bf16[32,160,2,128]{3,2,1,0:T(2,128)(2,1)S(1)} copy-done((bf16[32,160,2,128]{3,2,1,0:T(2,128)(2,1)S(1)}, bf16[32,160,2,128]{3,2,1,0:T(2,128)(2,1)}, u32[]{:S(2)}) %copy-start) | copy-done | bytes 2621464
  3.9 0.0 copy-start.4
  3.9 0.0 copy-start.1
  3.9 0.0 copy-start.2
  3.9 8.8 %shard_map.109 = (f32[72,768]{1,0:T(8,128)S(1)}, f32[3,16,256]{2,1,0:T(8,128)S(1)}, bf16[32,160,128]{2,1,0:T(8,128)(2,1)S(1)}, bf16[32,160,128]{2,1,0:T(8,128)(2,1)}) custom-call(bf16[10240,128]{1,0:T(8,128)(2,1)S(1)} %bitcast.13, f32[24,256]{1,0:T(8,128)S(1)} %concatenate.3.small_ref), custom_call_target="tpu_custom_call" | custom-call | flops 100000000 | bytes 8000000 | tf_op jit(solution)/shard_map/pallas_call | solution.py:365
  12.8 1.4 %collective-permute-start = (bf16[32,160,128]{2,1,0:T(8,128)(2,1)}, bf16[32,160,128]{2,1,0:T(8,128)(2,1)S(1)}, u32[]{:S(2)}, u32[]{:S(2)}) collective-permute-start(bf16[32,160,128]{2,1,0:T(8,128)(2,1)} %get-tuple-element.13), channel_id=1, source_target_pairs={{0,16},{16,0},{1,17},{17,1},{2,18},{18,2},{3,19},{19,3},{4,20},{20... | collective-permute-start | bytes 3932168 | tf_op jit(solution)/shard_map/ppermute | solution.py:756
  14.2 0.0 copy-done.4
  14.2 0.1 broadcast_in_dim.37
  14.3 0.0 copy-done.1
  14.3 0.0 copy-done.2
  14.3 0.0 copy-start.3
  14.4 23.2 %shard_map.110 = (f32[2560,128]{1,0:T(8,128)S(1)}, f32[2048,128]{1,0:T(8,128)S(1)}, f32[1,128]{1,0:T(1,128)S(1)}) custom-call(f32[72,768]{1,0:T(8,128)S(1)} %get-tuple-element.14.pool_ref, s32[32,128]{1,0:T(8,128)S(1)} %bitcast.14, s32[1,128]{1,0:T(1,128)S(1)} %copy-done.2, f32[1,128]{1,0:T(1,128)S(1)} %get-tuple-element.25.row_ref, ...), custom_call_target="tpu_custom_call" | custom-call | flops 2000000000 | bytes 200000000 | tf_op jit(solution)/shard_map/pallas_call | solution.py:236
  37.5 0.0 copy-done.3
  37.6 0.1 multiply_exponential_fusion
  37.7 0.1 broadcast_select_fusion.loss_ref
  37.8 5.6 %collective-permute-done.other_ref = bf16[32,160,128]{2,1,0:T(8,128)(2,1)S(1)} collective-permute-done((bf16[32,160,128]{2,1,0:T(8,128)(2,1)}, bf16[32,160,128]{2,1,0:T(8,128)(2,1)S(1)}, u32[]{:S(2)}, u32[]{:S(2)}) %collective-permute-start) | collective-permute-done | bytes 1310752 | tf_op jit(solution)/shard_map/ppermute | solution.py:756
  43.4 69.0 %shard_map.111 = bf16[10240,128]{1,0:T(8,128)(2,1)S(1)} custom-call(bf16[32,160,128]{2,1,0:T(8,128)(2,1)S(1)} %get-tuple-element.12.mine_ref, bf16[32,160,128]{2,1,0:T(8,128)(2,1)S(1)} %collective-permute-done.other_ref, f32[2560,128]{1,0:T(8,128)S(1)} %get-tuple-element.15.dev_ref, f32[2048,128]{1,0:T(8,128)S(1)} %get-tuple-element.16.mix_ref, ...), custom_call_target="tpu_custom_call" | custom-call | flops 1000000000 | bytes 10000000 | tf_op jit(solution)/shard_map/pallas_call | solution.py:617
  112.4 1.5 %copy.17 = bf16[32,160,2,128]{3,2,1,0:T(2,128)(2,1)} copy(bf16[32,160,2,128]{3,2,1,0:T(2,128)(2,1)S(1)} %bitcast.12) | data formatting | bytes 5242880
  (8 shorter events, 0.1 us)
Async XLA Ops:
  2.2 1.7 %copy-start = (bf16[32,160,2,128]{3,2,1,0:T(2,128)(2,1)S(1)}, bf16[32,160,2,128]{3,2,1,0:T(2,128)(2,1)}, u32[]{:S(2)}) copy-start(bf16[32,160,2,128]{3,2,1,0:T(2,128)(2,1)} %param.11) | copy-start | bytes 7864324
  3.9 10.2 %copy-start.4 = (f32[40]{0:T(128)S(1)}, f32[40]{0:T(128)}, u32[]{:S(2)}) copy-start(f32[40]{0:T(128)} %param.20) | copy-start | bytes 484
  3.9 10.4 %copy-start.1 = (s32[1,128,32]{1,2,0:T(8,128)S(1)}, s32[1,128,32]{1,2,0:T(8,128)}, u32[]{:S(2)}) copy-start(s32[1,128,32]{1,2,0:T(8,128)} %param.16) | copy-start | bytes 49156
  3.9 10.4 %copy-start.2 = (s32[1,128]{1,0:T(1,128)S(1)}, s32[1,128]{1,0:T(1,128)}, u32[]{:S(2)}) copy-start(s32[1,128]{1,0:T(1,128)} %cnt_ref.1) | copy-start | bytes 1540
  12.8 30.6 %collective-permute-start = (bf16[32,160,128]{2,1,0:T(8,128)(2,1)}, bf16[32,160,128]{2,1,0:T(8,128)(2,1)S(1)}, u32[]{:S(2)}, u32[]{:S(2)}) collective-permute-start(bf16[32,160,128]{2,1,0:T(8,128)(2,1)} %get-tuple-element.13), channel_id=1, source_target_pairs={{0,16},{16,0},{1,17},{17,1},{2,18},{18,2},{3,19},{19,3},{4,20},{20... | collective-permute-start | bytes 3932168 | tf_op jit(solution)/shard_map/ppermute | solution.py:756
  14.3 23.2 %copy-start.3 = (f32[2,128]{1,0:T(2,128)S(1)}, f32[2,128]{1,0:T(2,128)}, u32[]{:S(2)}) copy-start(f32[2,128]{1,0:T(2,128)} %param.21) | copy-start | bytes 3076

commit v4 on v3

--- a/solution.py
+++ b/solution.py
@@ -15,8 +15,10 @@
 GROUP = 8
 PITCH = 40
 WIDTH = 16
-LAG = 3
-UNROLL = 4
+LAG = 6
+RELAY = 3
+QUAD = 4
+UNROLL = 8
 INTERPRET = False
 
 
@@ -434,8 +436,8 @@
 def finish_kernel(
     slots, width,
     mine_ref, other_ref, dev_ref, mix_ref, keep_ref, edge_ref, loss_ref, out_ref,
-    rows, away, south, north, anomaly, mapped, mean_ref, coef, weave,
-    away_sent, away_come, edge_sent, edge_come,
+    rows, away, south, north, held_ref, anomaly, mapped, mean_ref, coef, weave,
+    away_sent, away_come, edge_sent, edge_come, held_sent, held_come,
 ):
     share, fields, _ = mine_ref.shape
     members = 2 * share
@@ -445,12 +447,26 @@
     mesh_id = pl.DeviceIdType.MESH
     exists = (place > 0, place + 1 < count)
     sides = ((1 - me, place), (me, place - 1), (me, place + 1))
+    relays = count % QUAD == 0 and count > QUAD
+    floors, floor, corner = count // QUAD, place // QUAD, place % QUAD
+    near, far = corner == 0, corner == QUAD - 1
+    across = (me, jnp.where(far, place - (QUAD - 1), place + (QUAD - 1)))
+    ahead = (me, jnp.where(far, place - QUAD, place + QUAD))
+    behind = (me, jnp.where(far, place + QUAD, place - QUAD))
+    goes = jnp.where(far, floor > 0, floor < floors - 1)
+    comes = jnp.where(far, floor < floors - 1, floor > 0)
     barrier = pltpu.get_barrier_semaphore()
     pl.semaphore_signal(barrier, inc=1, device_id=sides[0], device_id_type=mesh_id)
     for side in range(2):
         @pl.when(exists[side])
         def _():
             pl.semaphore_signal(barrier, inc=1, device_id=sides[1 + side], device_id_type=mesh_id)
+
+    if relays:
+        for there, device in ((True, across), (goes, ahead), (comes, behind)):
+            @pl.when((near | far) & there)
+            def _():
+                pl.semaphore_signal(barrier, inc=1, device_id=device, device_id_type=mesh_id)
 
     for side, buffer in enumerate((south, north)):
         @pl.when(jnp.logical_not(exists[side]))
@@ -480,7 +496,44 @@
                 coef[6 * at + n, pl.ds(piece * GROUP, GROUP), :] = value
 
     greeted = 1 + exists[0].astype(jnp.int32) + exists[1].astype(jnp.int32)
+    if relays:
+        more = 1 + goes.astype(jnp.int32) + comes.astype(jnp.int32)
+        greeted = greeted + jnp.where(near | far, more, 0)
     pl.semaphore_wait(barrier, greeted)
+
+    def share_of(r, q, part):
+        return (2 * r + q % 2) * floors < 4 * part
+
+    def detours(side, r, q):
+        if side:
+            return far & share_of(r, q, floors - 1 - floor)
+        return near & share_of(r, q, floor)
+
+    def hand_over(side, r, q):
+        return pltpu.make_async_remote_copy(
+            src_ref=rows.at[r, q], dst_ref=held_ref.at[r, q],
+            send_sem=edge_sent.at[side, r, q], recv_sem=held_come.at[r, q],
+            device_id=across, device_id_type=mesh_id,
+        )
+
+    def hand_on(side, r, q):
+        return pltpu.make_async_remote_copy(
+            src_ref=held_ref.at[r, q], dst_ref=(north, south)[side].at[r, q],
+            send_sem=held_sent.at[r, q], recv_sem=edge_come.at[side, r, q],
+            device_id=ahead, device_id_type=mesh_id,
+        )
+
+    def relayed(side, r, q):
+        if side:
+            return near & share_of(r, q, floors - 1 - floor)
+        return far & share_of(r, q, floor)
+
+    def relay(r, q):
+        for side in range(2):
+            @pl.when(relayed(side, r, q))
+            def _():
+                hand_over(side, r, q).wait_recv()
+                hand_on(side, r, q).start()
 
     def swap(q):
         return pltpu.make_async_remote_copy(
@@ -498,7 +551,16 @@
 
     def pass_both(r, q):
         for side in range(2):
-            @pl.when(exists[side])
+            if not relays:
+                pl.when(exists[side])(pass_on(side, r, q).start)
+                continue
+            turn = detours(side, r, q)
+
+            @pl.when(turn)
+            def _():
+                hand_over(side, r, q).start()
+
+            @pl.when(exists[side] & jnp.logical_not(turn))
             def _():
                 pass_on(side, r, q).start()
 
@@ -525,7 +587,7 @@
             lambda i, first, r: dev_ref[pl.ds(i * PITCH + first + r, 1), :],
             lambda i: anomaly[i], members, slots, width, to_mapped, group=group,
         )
-        for part in (1, 0):
+        for part in (0, 1):
             base = part * share
 
             def to_out(first, sums, base=base, part=part):
@@ -551,8 +613,9 @@
 
         def along(at, low, middle, high):
             now = coef[6 * at] * middle + coef[6 * at + 1] * high + coef[6 * at + 2] * low
-            east = pltpu.roll(now, LANES - 1, 1)
-            west = pltpu.roll(now, 1, 1)
+            thin = now.astype(jnp.bfloat16)
+            east = pltpu.roll(thin, LANES - 1, 1).astype(jnp.float32)
+            west = pltpu.roll(thin, 1, 1).astype(jnp.float32)
             return coef[6 * at + 3] * now + coef[6 * at + 4] * east + coef[6 * at + 5] * west
 
         def several(n, carry):
@@ -581,6 +644,12 @@
             swap(q - 1).wait_recv()
             pass_both(1 - me, q - 1)
 
+        if relays:
+            @pl.when((q >= RELAY) & (q - RELAY < chunks))
+            def _():
+                relay(me, q - RELAY)
+                relay(1 - me, q - RELAY)
+
         @pl.when((q >= LAG) & (q - LAG < chunks))
         def _():
             for side in range(2):
@@ -602,6 +671,12 @@
             def _():
                 for r in range(2):
                     pass_on(side, r, q).wait_send()
+
+            if relays:
+                for r in range(2):
+                    @pl.when(relayed(side, r, q))
+                    def _():
+                        hand_on(side, r, q).wait_send()
 
         return carry
 
@@ -624,6 +699,7 @@
             pltpu.VMEM(piece, jnp.bfloat16),
             pltpu.VMEM((2,) + piece, jnp.bfloat16),
             pltpu.VMEM((2,) + piece, jnp.bfloat16),
+            pltpu.VMEM((2,) + piece, jnp.bfloat16),
             pltpu.VMEM((2 * share, width, LANES), jnp.float32),
             pltpu.VMEM((slots, width, LANES), jnp.float32),
             pltpu.VMEM((width, LANES), jnp.float32),
@@ -633,6 +709,8 @@
             pltpu.SemaphoreType.DMA((chunks,)),
             pltpu.SemaphoreType.DMA((2, 2, chunks)),
             pltpu.SemaphoreType.DMA((2, 2, chunks)),
+            pltpu.SemaphoreType.DMA((2, chunks)),
+            pltpu.SemaphoreType.DMA((2, chunks)),
         ],
         compiler_params=pltpu.CompilerParams(
             vmem_limit_bytes=40 * 1024 * 1024, collective_id=1, has_side_effects=True

time: 114 us -> 105 us (0.921)
  Pallas kernels: 101 us -> 91.8 us
    pallas_call x1, Pallas kernels: 69 us -> 59.8 us  [finish(): pl.pallas_call(functools.partial(finish_kernel, slots, width), in_specs=[...]
  transfers between devices with their start and end apart: 1 -> 1, of which waited for: 1 -> 1; matrix products, arithmetic and copies ran while one was open for 0% -> 0% of each run, Pallas kernels for 20% -> 22%
where the time goes in v4:
time: 105 us
  Pallas kernels  91.8 us (87%)
  waiting for transfers between devices  5.58 us (5%)
  local copies, waits for them, and re-layouts  4.87 us (5%)
  starting transfers between devices  1.37 us (1%)
    pallas_call x1, Pallas kernels, finish(): pl.pallas_call(functools.partial(finish_kernel, slots, width), in_specs=[...  59.8 us
    pallas_call x1, Pallas kernels, solve_cells(): pl.pallas_call(functools.partial(weights_kernel, members, NEWTON, LOC), g...  23.2 us
    pallas_call x1, Pallas kernels, prepare(): pl.pallas_call(functools.partial(prep_kernel, rows, levels), in_specs=[vm...  8.84 us
    ppermute x1, waiting for transfers between devices, shards(): states = (mine, lax.ppermute(theirs, 'mem', swap))  5.58 us
    unnamed x11, local copies, waits for them, and re-layouts  3.25 us
  transfers between devices with their start and end apart: 1, of which 1 were waited for; matrix products, arithmetic and copies ran while one was open for 0% of the time, Pallas kernels for 22%

profile of v4, /device:TPU:17, one launch (start us, length us, event | category | flops | bytes accessed | tf_op | source)
XLA Modules:
  0.0 104.7 jit_solution(12901215503596785487)
XLA Ops:
  0.0 0.7 add_convert_fusion
  0.7 0.7 copy_bitcast_fusion
  1.4 0.8 concatenate.3.small_ref
  2.2 0.0 copy-start
  2.2 1.7 %copy-done = bf16[32,160,2,128]{3,2,1,0:T(2,128)(2,1)S(1)} copy-done((bf16[32,160,2,128]{3,2,1,0:T(2,128)(2,1)S(1)}, bf16[32,160,2,128]{3,2,1,0:T(2,128)(2,1)}, u32[]{:S(2)}) %copy-start) | copy-done | bytes 2621464
  3.9 0.0 copy-start.4
  3.9 0.0 copy-start.1
  3.9 0.0 copy-start.2
  3.9 8.8 %shard_map.109 = (f32[72,768]{1,0:T(8,128)S(1)}, f32[3,16,256]{2,1,0:T(8,128)S(1)}, bf16[32,160,128]{2,1,0:T(8,128)(2,1)S(1)}, bf16[32,160,128]{2,1,0:T(8,128)(2,1)}) custom-call(bf16[10240,128]{1,0:T(8,128)(2,1)S(1)} %bitcast.13, f32[24,256]{1,0:T(8,128)S(1)} %concatenate.3.small_ref), custom_call_target="tpu_custom_call" | custom-call | flops 100000000 | bytes 8000000 | tf_op jit(solution)/shard_map/pallas_call | solution.py:367
  12.8 1.4 %collective-permute-start = (bf16[32,160,128]{2,1,0:T(8,128)(2,1)}, bf16[32,160,128]{2,1,0:T(8,128)(2,1)S(1)}, u32[]{:S(2)}, u32[]{:S(2)}) collective-permute-start(bf16[32,160,128]{2,1,0:T(8,128)(2,1)} %get-tuple-element.13), channel_id=1, source_target_pairs={{0,16},{16,0},{1,17},{17,1},{2,18},{18,2},{3,19},{19,3},{4,20},{20... | collective-permute-start | bytes 3932168 | tf_op jit(solution)/shard_map/ppermute | solution.py:834
  14.2 0.0 copy-done.4
  14.2 0.1 broadcast_in_dim.37
  14.3 0.0 copy-done.1
  14.3 0.0 copy-done.2
  14.3 0.0 copy-start.3
  14.4 23.2 %shard_map.110 = (f32[2560,128]{1,0:T(8,128)S(1)}, f32[2048,128]{1,0:T(8,128)S(1)}, f32[1,128]{1,0:T(1,128)S(1)}) custom-call(f32[72,768]{1,0:T(8,128)S(1)} %get-tuple-element.14.pool_ref, s32[32,128]{1,0:T(8,128)S(1)} %bitcast.14, s32[1,128]{1,0:T(1,128)S(1)} %copy-done.2, f32[1,128]{1,0:T(1,128)S(1)} %get-tuple-element.25.row_ref, ...), custom_call_target="tpu_custom_call" | custom-call | flops 2000000000 | bytes 200000000 | tf_op jit(solution)/shard_map/pallas_call | solution.py:238
  37.5 0.0 copy-done.3
  37.6 0.1 multiply_exponential_fusion
  37.7 0.1 broadcast_select_fusion.loss_ref
  37.8 5.6 %collective-permute-done.other_ref = bf16[32,160,128]{2,1,0:T(8,128)(2,1)S(1)} collective-permute-done((bf16[32,160,128]{2,1,0:T(8,128)(2,1)}, bf16[32,160,128]{2,1,0:T(8,128)(2,1)S(1)}, u32[]{:S(2)}, u32[]{:S(2)}) %collective-permute-start) | collective-permute-done | bytes 1310752 | tf_op jit(solution)/shard_map/ppermute | solution.py:834
  43.4 59.8 %shard_map.111 = bf16[10240,128]{1,0:T(8,128)(2,1)S(1)} custom-call(bf16[32,160,128]{2,1,0:T(8,128)(2,1)S(1)} %get-tuple-element.12.mine_ref, bf16[32,160,128]{2,1,0:T(8,128)(2,1)S(1)} %collective-permute-done.other_ref, f32[2560,128]{1,0:T(8,128)S(1)} %get-tuple-element.15.dev_ref, f32[2048,128]{1,0:T(8,128)S(1)} %get-tuple-element.16.mix_ref, ...), custom_call_target="tpu_custom_call" | custom-call | flops 1000000000 | bytes 10000000 | tf_op jit(solution)/shard_map/pallas_call | solution.py:692
  103.2 1.5 %copy.17 = bf16[32,160,2,128]{3,2,1,0:T(2,128)(2,1)} copy(bf16[32,160,2,128]{3,2,1,0:T(2,128)(2,1)S(1)} %bitcast.12) | data formatting | bytes 5242880
  (8 shorter events, 0.1 us)
Async XLA Ops:
  2.2 1.7 %copy-start = (bf16[32,160,2,128]{3,2,1,0:T(2,128)(2,1)S(1)}, bf16[32,160,2,128]{3,2,1,0:T(2,128)(2,1)}, u32[]{:S(2)}) copy-start(bf16[32,160,2,128]{3,2,1,0:T(2,128)(2,1)} %param.11) | copy-start | bytes 7864324
  3.9 10.2 %copy-start.4 = (f32[40]{0:T(128)S(1)}, f32[40]{0:T(128)}, u32[]{:S(2)}) copy-start(f32[40]{0:T(128)} %param.20) | copy-start | bytes 484
  3.9 10.4 %copy-start.1 = (s32[1,128,32]{1,2,0:T(8,128)S(1)}, s32[1,128,32]{1,2,0:T(8,128)}, u32[]{:S(2)}) copy-start(s32[1,128,32]{1,2,0:T(8,128)} %param.16) | copy-start | bytes 49156
  3.9 10.4 %copy-start.2 = (s32[1,128]{1,0:T(1,128)S(1)}, s32[1,128]{1,0:T(1,128)}, u32[]{:S(2)}) copy-start(s32[1,128]{1,0:T(1,128)} %cnt_ref.1) | copy-start | bytes 1540
  12.8 30.6 %collective-permute-start = (bf16[32,160,128]{2,1,0:T(8,128)(2,1)}, bf16[32,160,128]{2,1,0:T(8,128)(2,1)S(1)}, u32[]{:S(2)}, u32[]{:S(2)}) collective-permute-start(bf16[32,160,128]{2,1,0:T(8,128)(2,1)} %get-tuple-element.13), channel_id=1, source_target_pairs={{0,16},{16,0},{1,17},{17,1},{2,18},{18,2},{3,19},{19,3},{4,20},{20... | collective-permute-start | bytes 3932168 | tf_op jit(solution)/shard_map/ppermute | solution.py:834
  14.3 23.2 %copy-start.3 = (f32[2,128]{1,0:T(2,128)S(1)}, f32[2,128]{1,0:T(2,128)}, u32[]{:S(2)}) copy-start(f32[2,128]{1,0:T(2,128)} %param.21) | copy-start | bytes 3076

commit v5 on v4

--- a/solution.py
+++ b/solution.py
@@ -17,6 +17,7 @@
 WIDTH = 16
 LAG = 6
 RELAY = 3
+LATE = 3
 QUAD = 4
 UNROLL = 8
 INTERPRET = False
@@ -260,12 +261,49 @@
     )(pool, idx, counts, rows, cols)
 
 
-def prep_kernel(rows, levels, ens_ref, small_ref, pool_ref, edge_ref, mine_ref, theirs_ref, block, land, spread, send_sems, recv_sems):
-    share, fields, _ = mine_ref.shape
-    observed = small_ref.shape[1]
+def split_kernel(rows, levels, flat_ref, mine_ref, early_ref, late_ref, lowest_ref, spread):
+    me = lax.axis_index("mem")
+    batch, fields, _ = mine_ref.shape
+    species = fields // levels
     span = fields * rows
-    facts = small_ref.shape[0]
-    species = fields // levels
+    for slot in range(batch):
+        spread[slot] = flat_ref[pl.ds(slot * span, span), :].astype(jnp.float32)
+        mine_ref[slot] = spread[slot, pl.ds(me, fields, stride=rows), :].astype(jnp.bfloat16)
+        theirs = spread[slot, pl.ds(1 - me, fields, stride=rows), :].astype(jnp.bfloat16)
+        early_ref[slot] = theirs[: early_ref.shape[1]]
+        late_ref[slot] = theirs[early_ref.shape[1] :]
+        lowest_ref[slot] = jnp.concatenate(
+            [spread[slot, pl.ds(r, species, stride=rows * levels), :] for r in range(rows)], axis=0
+        ).astype(jnp.bfloat16)
+
+
+def separate(flat, share, fields, rows, levels):
+    span = fields * rows
+    block = lambda height: pl.BlockSpec((UNROLL, height, LANES), lambda n: (n, 0, 0))
+    out = lambda height: jax.ShapeDtypeStruct((share, height, LANES), jnp.bfloat16)
+    late = LATE * WIDTH
+    heights = (fields, fields - late, late, rows * fields // levels)
+    return pl.pallas_call(
+        functools.partial(split_kernel, rows, levels),
+        grid=(share // UNROLL,),
+        in_specs=[pl.BlockSpec((UNROLL * span, LANES), lambda n: (n, 0))],
+        out_specs=[block(height) for height in heights],
+        out_shape=[out(height) for height in heights],
+        scratch_shapes=[pltpu.VMEM((UNROLL, span, LANES), jnp.float32)],
+        compiler_params=pltpu.CompilerParams(vmem_limit_bytes=16 * 1024 * 1024),
+        cost_estimate=pl.CostEstimate(flops=10**7, bytes_accessed=6 * 10**6, transcendentals=0),
+        interpret=INTERPRET,
+    )(flat)
+
+
+def prep_kernel(
+    rows, species,
+    lowest_ref, value_ref, error_ref, cell_ref, species_ref, courant_x_ref, courant_y_ref,
+    pool_ref, edge_ref, found, block, facts_ref, land, land_facts, send_sems, recv_sems, facts_sent, facts_come,
+):
+    share = lowest_ref.shape[0]
+    observed = value_ref.shape[1]
+    levels = courant_x_ref.shape[0] // rows
     me, place, count = lax.axis_index("mem"), lax.axis_index("space"), lax.axis_size("space")
 
     def exists(step):
@@ -289,24 +327,29 @@
 
         guard(step, greet)
 
-    block[pl.ds(share, facts), :] = small_ref[...]
-    hot = jnp.where(
-        lax.broadcasted_iota(jnp.int32, (LANES, observed), 0).astype(jnp.float32) == small_ref[3:4, :], 1.0, 0.0
-    ).astype(jnp.bfloat16)
-    wanted = lax.broadcasted_iota(jnp.int32, (rows * species, observed), 0).astype(jnp.float32) == small_ref[4:5, :]
+    cell = cell_ref[...]
+    row, column = lax.shift_right_logical(cell, LANES.bit_length() - 1), cell & (LANES - 1)
+    facts_ref[pl.ds(0, GROUP), :] = jnp.zeros((GROUP, observed), jnp.float32)
+    facts = (value_ref[...], error_ref[...], row.astype(jnp.float32), column.astype(jnp.float32))
+    for n, fact in enumerate(facts):
+        facts_ref[pl.ds(n, 1), :] = fact
+    for n, courant in enumerate((courant_x_ref, courant_y_ref)):
+        for copy in range(GROUP // levels):
+            for r in range(rows):
+                start = (n + 1) * GROUP + copy * levels
+                facts_ref[pl.ds(start, levels), pl.ds(r * LANES, LANES)] = courant[pl.ds(r, levels, stride=rows), :]
+    hot = jnp.where(lax.broadcasted_iota(jnp.int32, (LANES, observed), 0) == column, 1.0, 0.0).astype(jnp.bfloat16)
+    wanted = lax.broadcasted_iota(jnp.int32, (rows * species, observed), 0) == row * species + species_ref[...]
 
     def look(n, carry):
         for slot in range(UNROLL):
             i = UNROLL * n + slot
-            spread[slot] = ens_ref[pl.ds(pl.multiple_of(i * span, span), span), :].astype(jnp.float32)
-            lowest = jnp.concatenate(
-                [spread[slot, pl.ds(r, species, stride=rows * levels), :] for r in range(rows)], axis=0
-            )
-            got = jnp.dot(lowest.astype(jnp.bfloat16), hot, preferred_element_type=jnp.float32)
-            block[pl.ds(i, 1), :] = jnp.sum(jnp.where(wanted, got, 0.0), axis=0, keepdims=True)
+            got = jnp.dot(lowest_ref[i], hot, preferred_element_type=jnp.float32)
+            found[pl.ds(i, 1), :] = jnp.sum(jnp.where(wanted, got, 0.0), axis=0, keepdims=True)
         return carry
 
     lax.fori_loop(0, share // UNROLL, look, 0)
+    block[...] = found[...].astype(jnp.bfloat16)
 
     greeted = 1 + 2 * exists(-1).astype(jnp.int32) + 2 * exists(1).astype(jnp.int32)
     pl.semaphore_wait(barrier, greeted)
@@ -319,74 +362,79 @@
             device_id=target(flip, step), device_id_type=pl.DeviceIdType.MESH,
         )
 
+    def copy_facts(step):
+        return pltpu.make_async_remote_copy(
+            src_ref=facts_ref, dst_ref=land_facts.at[1 - step],
+            send_sem=facts_sent.at[1 - step], recv_sem=facts_come.at[1 - step],
+            device_id=(me, place + step), device_id_type=pl.DeviceIdType.MESH,
+        )
+
     for n, (flip, step) in enumerate(ways):
         guard(step, lambda n=n: copy(n).start())
-
-    def split(n, carry):
-        for slot in range(UNROLL):
-            i = UNROLL * n + slot
-            spread[slot] = ens_ref[pl.ds(pl.multiple_of(i * span, span), span), :].astype(jnp.float32)
-            mine_ref[i] = spread[slot, pl.ds(me, fields, stride=rows), :].astype(jnp.bfloat16)
-            theirs_ref[i] = spread[slot, pl.ds(1 - me, fields, stride=rows), :].astype(jnp.bfloat16)
-        return carry
-
-    lax.fori_loop(0, share // UNROLL, split, 0)
-
-    for n, (flip, step) in enumerate(ways):
-        def arrive(n=n):
-            copy(n).wait_send()
-
-        guard(step, arrive)
+    for step in (-1, 1):
+        guard(step, lambda step=step: copy_facts(step).start())
+    for step in (-1, 1):
+        def blank(step=step):
+            land[1 + step] = jnp.zeros_like(land[1 + step])
+            land_facts[1 + step] = jnp.zeros_like(land_facts[1 + step])
+
+        pl.when(jnp.logical_not(exists(step)))(blank)
     for n, (flip, step) in enumerate(ways):
         def landed(n=n):
             copy(n).wait_recv()
 
         guard(-step, landed)
     for step in (-1, 1):
-        def blank(step=step):
-            land[1 + step] = jnp.zeros_like(land[1 + step])
-
-        pl.when(jnp.logical_not(exists(step)))(blank)
+        guard(-step, lambda step=step: copy_facts(step).wait_recv())
     line = lax.broadcasted_iota(jnp.int32, (GROUP, observed), 0)
     for part in range(3):
-        own = block[...] if part == 1 else land[part, 0]
         lanes = pl.ds(part * observed, observed)
-        pool_ref[pl.ds(0, share), lanes] = own[:share]
-        pool_ref[pl.ds(share, share), lanes] = land[part, 1, pl.ds(0, share), :]
-        pool_ref[pl.ds(2 * share, GROUP), lanes] = own[share : share + GROUP] + jnp.where(
+        own = found[...] if part == 1 else land[part, 0].astype(jnp.float32)
+        facts = (facts_ref if part == 1 else land_facts.at[part])[...]
+        pool_ref[pl.ds(0, share), lanes] = own
+        pool_ref[pl.ds(share, share), lanes] = land[part, 1].astype(jnp.float32)
+        pool_ref[pl.ds(2 * share, GROUP), lanes] = facts[:GROUP] + jnp.where(
             line == 2, float(rows * (part - 1)), 0.0
         )
-        edge_ref[part] = own[share + GROUP :]
-
-
-def prepare(flat, small, members, fields, rows, levels):
-    share = members // 2
-    observed = small.shape[1]
-    high = share + small.shape[0]
+        edge_ref[part] = facts[GROUP:]
+    for n, (flip, step) in enumerate(ways):
+        def sent(n=n):
+            copy(n).wait_send()
+
+        guard(step, sent)
+    for step in (-1, 1):
+        guard(step, lambda step=step: copy_facts(step).wait_send())
+
+
+def prepare(lowest, facts, courants, rows, species):
+    share = lowest.shape[0]
+    observed = facts[0].shape[1]
     vmem = pl.BlockSpec(memory_space=pltpu.VMEM)
     return pl.pallas_call(
-        functools.partial(prep_kernel, rows, levels),
-        in_specs=[vmem] * 2,
-        out_specs=[vmem] * 4,
+        functools.partial(prep_kernel, rows, species),
+        in_specs=[vmem] * 7,
+        out_specs=[vmem] * 2,
         out_shape=[
-            jax.ShapeDtypeStruct((members + GROUP, 3 * observed), jnp.float32),
-            jax.ShapeDtypeStruct((3, small.shape[0] - GROUP, observed), jnp.float32),
-            jax.ShapeDtypeStruct((share, fields, LANES), jnp.bfloat16),
-            jax.ShapeDtypeStruct((share, fields, LANES), jnp.bfloat16),
+            jax.ShapeDtypeStruct((2 * share + GROUP, 3 * observed), jnp.float32),
+            jax.ShapeDtypeStruct((3, 2 * GROUP, observed), jnp.float32),
         ],
         scratch_shapes=[
-            pltpu.VMEM((high, observed), jnp.float32),
-            pltpu.VMEM((3, 2, high, observed), jnp.float32),
-            pltpu.VMEM((UNROLL, fields * rows, LANES), jnp.float32),
+            pltpu.VMEM((share, observed), jnp.float32),
+            pltpu.VMEM((share, observed), jnp.bfloat16),
+            pltpu.VMEM((3 * GROUP, observed), jnp.float32),
+            pltpu.VMEM((3, 2, share, observed), jnp.bfloat16),
+            pltpu.VMEM((3, 3 * GROUP, observed), jnp.float32),
             pltpu.SemaphoreType.DMA((5,)),
             pltpu.SemaphoreType.DMA((3, 2)),
+            pltpu.SemaphoreType.DMA((3,)),
+            pltpu.SemaphoreType.DMA((3,)),
         ],
         compiler_params=pltpu.CompilerParams(
-            vmem_limit_bytes=32 * 1024 * 1024, collective_id=0, has_side_effects=True
+            vmem_limit_bytes=16 * 1024 * 1024, collective_id=0, has_side_effects=True
         ),
-        cost_estimate=pl.CostEstimate(flops=10**8, bytes_accessed=8 * 10**6, transcendentals=0),
+        cost_estimate=pl.CostEstimate(flops=10**8, bytes_accessed=10**6, transcendentals=0),
         interpret=INTERPRET,
-    )(flat, small)
+    )(lowest, *facts, *courants)
 
 
 def analysis_kernel(parts, slots, *refs):
@@ -435,13 +483,14 @@
 
 def finish_kernel(
     slots, width,
-    mine_ref, other_ref, dev_ref, mix_ref, keep_ref, edge_ref, loss_ref, out_ref,
-    rows, away, south, north, held_ref, anomaly, mapped, mean_ref, coef, weave,
-    away_sent, away_come, edge_sent, edge_come, held_sent, held_come,
+    mine_ref, other_ref, theirs_ref, dev_ref, mix_ref, keep_ref, edge_ref, loss_ref, out_ref,
+    rows, away, south, north, held_ref, late_ref, anomaly, mapped, mean_ref, coef, weave,
+    away_sent, away_come, edge_sent, edge_come, held_sent, held_come, late_sent, late_come,
 ):
     share, fields, _ = mine_ref.shape
     members = 2 * share
     chunks = fields // width
+    early = other_ref.shape[1] // width
     group = 2 * LANES // width
     me, place, count = lax.axis_index("mem"), lax.axis_index("space"), lax.axis_size("space")
     mesh_id = pl.DeviceIdType.MESH
@@ -564,20 +613,44 @@
             def _():
                 pass_on(side, r, q).start()
 
+    def follow(n):
+        return pltpu.make_async_remote_copy(
+            src_ref=theirs_ref.at[:, pl.ds(pl.multiple_of(n * width, width), width), :], dst_ref=late_ref.at[n],
+            send_sem=late_sent.at[n], recv_sem=late_come.at[n],
+            device_id=sides[0], device_id_type=mesh_id,
+        )
+
     def analyse_chunk(q):
         cut = pl.ds(pl.multiple_of(q * width, width), width)
-        total = jnp.zeros((width, LANES), jnp.float32)
-        for state in (mine_ref, other_ref):
-            total = lax.fori_loop(
-                0, share, lambda i, t, s=state: t + s[i, cut, :].astype(jnp.float32), total, unroll=4
-            )
-        mean_ref[...] = total * (1.0 / members)
-        for part, state in enumerate((mine_ref, other_ref)):
-            def subtract(i, carry, s=state, base=part * share):
-                anomaly[base + i] = s[i, cut, :].astype(jnp.float32) - mean_ref[...]
-                return carry
-
-            lax.fori_loop(0, share, subtract, 0, unroll=4)
+        zero = jnp.zeros((width, LANES), jnp.float32)
+
+        def fill(load, base):
+            def one(i, total):
+                value = load(i).astype(jnp.float32)
+                anomaly[base + i] = value
+                return total + value
+
+            return lax.fori_loop(0, share, one, zero, unroll=4)
+
+        mean_ref[...] = fill(lambda i: mine_ref[i, cut, :], 0)
+
+        @pl.when(q < early)
+        def _():
+            mean_ref[...] += fill(lambda i: other_ref[i, cut, :], share)
+
+        @pl.when(q >= early)
+        def _():
+            follow(q - early).wait_recv()
+            mean_ref[...] += fill(lambda i: late_ref[q - early, i], share)
+
+        mean = mean_ref[...] * (1.0 / members)
+        mean_ref[...] = mean
+
+        def subtract(i, carry):
+            anomaly[i] = anomaly[i] - mean
+            return carry
+
+        lax.fori_loop(0, members, subtract, 0, unroll=8)
 
         def to_mapped(first, sums):
             for r in range(group):
@@ -605,6 +678,10 @@
             )
             if part:
                 swap(q).start()
+
+                @pl.when(q < chunks - early)
+                def _():
+                    follow(q).start()
             else:
                 pass_both(me, q)
 
@@ -666,6 +743,11 @@
 
     def drain(q, carry):
         swap(q).wait_send()
+
+        @pl.when(q < chunks - early)
+        def _():
+            follow(q).wait_send()
+
         for side in range(2):
             @pl.when(exists[side])
             def _():
@@ -683,15 +765,16 @@
     lax.fori_loop(0, chunks, drain, 0)
 
 
-def finish(mine, other, dev, mix, keep, edge, loss, slots, rows):
+def finish(mine, other, theirs, dev, mix, keep, edge, loss, slots, rows):
     share, fields, _ = mine.shape
     width = WIDTH
     chunks = fields // width
+    late = theirs.shape[1] // width
     vmem = pl.BlockSpec(memory_space=pltpu.VMEM)
     piece = (chunks, share, width, LANES)
     return pl.pallas_call(
         functools.partial(finish_kernel, slots, width),
-        in_specs=[vmem] * 7,
+        in_specs=[vmem] * 8,
         out_specs=vmem,
         out_shape=jax.ShapeDtypeStruct((share * fields * rows, LANES), jnp.bfloat16),
         scratch_shapes=[
@@ -700,6 +783,7 @@
             pltpu.VMEM((2,) + piece, jnp.bfloat16),
             pltpu.VMEM((2,) + piece, jnp.bfloat16),
             pltpu.VMEM((2,) + piece, jnp.bfloat16),
+            pltpu.VMEM((late,) + piece[1:], jnp.bfloat16),
             pltpu.VMEM((2 * share, width, LANES), jnp.float32),
             pltpu.VMEM((slots, width, LANES), jnp.float32),
             pltpu.VMEM((width, LANES), jnp.float32),
@@ -711,13 +795,15 @@
             pltpu.SemaphoreType.DMA((2, 2, chunks)),
             pltpu.SemaphoreType.DMA((2, chunks)),
             pltpu.SemaphoreType.DMA((2, chunks)),
+            pltpu.SemaphoreType.DMA((late,)),
+            pltpu.SemaphoreType.DMA((late,)),
         ],
         compiler_params=pltpu.CompilerParams(
             vmem_limit_bytes=40 * 1024 * 1024, collective_id=1, has_side_effects=True
         ),
         cost_estimate=pl.CostEstimate(flops=10**9, bytes_accessed=10**7, transcendentals=0),
         interpret=INTERPRET,
-    )(mine, other, dev, mix, keep, edge, loss)
+    )(mine, other, theirs, dev, mix, keep, edge, loss)
 
 
 def analyse(states, dev, mix, keep, slots, first, count, width):
@@ -788,28 +874,21 @@
     slots = patch_index.shape[2]
     per_dev = tile_cells // groups
     paired = groups == 2 and tile_rows == 2 and columns == LANES
-    paired = paired and GROUP % levels == 0 and fields % WIDTH == 0 and species % GROUP == 0
+    paired = paired and GROUP % levels == 0 and fields % WIDTH == 0 and fields > 2 * LATE * WIDTH and species % GROUP == 0
     paired = paired and local_members % UNROLL == 0
     swap = [(0, 1), (1, 0)]
 
     if paired:
-        tall = GROUP // levels
-        small = jnp.concatenate(
-            [
-                obs_value,
-                obs_error,
-                (obs_cell // columns).astype(jnp.float32),
-                (obs_cell % columns).astype(jnp.float32),
-                (obs_cell // columns * species + obs_species).astype(jnp.float32),
-                jnp.zeros((GROUP - 5, obs_value.shape[1]), jnp.float32),
-            ]
-            + [courant_x.reshape(levels, tile_cells)] * tall
-            + [courant_y.reshape(levels, tile_cells)] * tall,
-            axis=0,
-        )
-        pool, edge, mine, theirs = prepare(
-            ensemble.reshape(-1, columns), small, members, fields, tile_rows, levels
-        )
+        mine, theirs, late, lowest = separate(
+            ensemble.reshape(-1, columns), local_members, fields, tile_rows, levels
+        )
+        pool, edge = prepare(
+            lowest,
+            (obs_value, obs_error, obs_cell, obs_species),
+            (courant_x.reshape(-1, columns), courant_y.reshape(-1, columns)),
+            tile_rows, species,
+        )
+        theirs, pool = lax.optimization_barrier((theirs, pool))
     else:
         surface = ensemble.reshape(local_members, species, levels, tile_cells)[:, :, 0]
         position = obs_species[0] * tile_cells + obs_cell[0]
@@ -856,7 +935,7 @@
     if paired:
         lowest = (jnp.arange(levels, dtype=jnp.int32) == 0)[None, None, :, None]
         factor = jnp.where(lowest, jnp.moveaxis(loss, 1, 0)[:, :, None], 1.0).reshape(tile_rows, fields, columns)
-        out = finish(*states, dev, mix, keep, edge, factor, slots, tile_rows)
+        out = finish(*states, late, dev, mix, keep, edge, factor, slots, tile_rows)
         return out.reshape(ensemble.shape)
 
     width = next(w for w in (32, 16, fields) if fields % w == 0)

time: 105 us -> 100 us (0.952)
  the two profiles are of different devices: /device:TPU:17 before, /device:TPU:15 now
where the time goes in v5:
time: 100 us
  Pallas kernels  95.8 us (96%)
  local copies, waits for them, and re-layouts  3.45 us (3%)
    pallas_call x1, Pallas kernels, finish(): pl.pallas_call(functools.partial(finish_kernel, slots, width), in_specs=[...  64.9 us
    pallas_call x1, Pallas kernels, solve_cells(): pl.pallas_call(functools.partial(weights_kernel, members, NEWTON, LOC), g...  23.2 us
    pallas_call x1, Pallas kernels, prepare(): pl.pallas_call(functools.partial(prep_kernel, rows, species), in_specs=[v...  5.39 us
    unnamed x23, local copies, waits for them, and re-layouts  3.3 us
    pallas_call x1, Pallas kernels, separate(): pl.pallas_call(functools.partial(split_kernel, rows, levels), grid=(share...  2.31 us
  transfers between devices with their start and end apart: 1, of which 0 were waited for; matrix products, arithmetic and copies ran while one was open for 0% of the time, Pallas kernels for 23%

profile of v5, /device:TPU:15, one launch (start us, length us, event | category | flops | bytes accessed | tf_op | source)
XLA Modules:
  0.0 100.2 jit_solution(7720449804912028184)
XLA Ops:
  0.0 1.8 %copy-done = bf16[32,160,2,128]{3,2,1,0:T(2,128)(2,1)S(1)} copy-done((bf16[32,160,2,128]{3,2,1,0:T(2,128)(2,1)S(1)}, bf16[32,160,2,128]{3,2,1,0:T(2,128)(2,1)}, u32[]{:S(2)}) %copy-start) | copy-done | bytes 2621464
  1.8 0.0 copy-start.6
  1.8 0.0 copy-start.10
  1.8 0.0 copy-start.7
  1.8 2.3 %shard_map.109 = (bf16[32,160,128]{2,1,0:T(8,128)(2,1)S(1)}, bf16[32,112,128]{2,1,0:T(8,128)(2,1)}, bf16[32,48,128]{2,1,0:T(8,128)(2,1)S(1)}, bf16[32,80,128]{2,1,0:T(8,128)(2,1)S(1)}) custom-call(bf16[10240,128]{1,0:T(8,128)(2,1)S(1)} %bitcast.9), custom_call_target="tpu_custom_call" | custom-call | flops 10000000 | bytes 6000000 | tf_op jit(solution)/shard_map/pallas_call | solution.py:286
  4.1 0.0 copy-done.3
  4.1 0.0 copy-done.1
  4.1 0.0 copy-done.2
  4.1 0.0 copy-done.4
  4.1 0.0 copy-done.5
  4.2 0.0 copy-done.6
  4.2 5.4 %shard_map.110 = (f32[72,768]{1,0:T(8,128)S(1)}, f32[3,16,256]{2,1,0:T(8,128)S(1)}) custom-call(bf16[32,80,128]{2,1,0:T(8,128)(2,1)S(1)} %get-tuple-element.18.lowest_ref, f32[1,256]{1,0:T(1,128)S(1)} %copy-done.3, f32[1,256]{1,0:T(1,128)S(1)} %copy-done.4, s32[1,256]{1,0:T(1,128)S(1)} %copy-done.5, s32[1,256]{1,0:T(1,128)S(1)} %copy-done.6, ...), custom_call_target="tpu_custom_call" | custom-call | flops 100000000 | bytes 1000000 | tf_op jit(solution)/shard_map/pallas_call | solution.py:413
  9.6 0.6 collective-permute-start
  10.2 0.1 broadcast_in_dim.33
  10.3 0.0 copy-done.8
  10.3 0.0 copy-done.7
  10.4 0.0 copy-start.9
  10.4 23.2 %shard_map.111 = (f32[2560,128]{1,0:T(8,128)S(1)}, f32[2048,128]{1,0:T(8,128)S(1)}, f32[1,128]{1,0:T(1,128)S(1)}) custom-call(f32[72,768]{1,0:T(8,128)S(1)} %get-tuple-element.22.pool_ref, s32[32,128]{1,0:T(8,128)S(1)} %bitcast.12, s32[1,128]{1,0:T(1,128)S(1)} %copy-done.8, f32[1,128]{1,0:T(1,128)S(1)} %get-tuple-element.28.row_ref, ...), custom_call_target="tpu_custom_call" | custom-call | flops 2000000000 | bytes 200000000 | tf_op jit(solution)/shard_map/pallas_call | solution.py:239
  33.6 0.0 copy-done.9
  33.6 0.1 multiply_exponential_fusion
  33.7 0.1 broadcast_select_fusion.loss_ref
  33.8 0.0 collective-permute-done.other_ref
  33.8 64.9 %shard_map.112 = bf16[10240,128]{1,0:T(8,128)(2,1)S(1)} custom-call(bf16[32,160,128]{2,1,0:T(8,128)(2,1)S(1)} %get-tuple-element.16.mine_ref, bf16[32,112,128]{2,1,0:T(8,128)(2,1)S(1)} %collective-permute-done.other_ref, bf16[32,48,128]{2,1,0:T(8,128)(2,1)S(1)} %get-tuple-element.21.theirs_ref, f32[2560,128]{1,0:T(8,128)S(1)} %get-tuple-element.23.dev_ref, ...), custom_call_target="tpu_custom_call" | custom-call | flops 1000000000 | bytes 10000000 | tf_op jit(solution)/shard_map/pallas_call | solution.py:775
  98.7 1.5 %copy.13 = bf16[32,160,2,128]{3,2,1,0:T(2,128)(2,1)} copy(bf16[32,160,2,128]{3,2,1,0:T(2,128)(2,1)S(1)} %bitcast.8) | data formatting | bytes 5242880
  (13 shorter events, 0.1 us)
Async XLA Ops:
  0.0 4.1 %copy-start.3 = (f32[1,256]{1,0:T(1,128)S(1)}, f32[1,256]{1,0:T(1,128)}, u32[]{:S(2)}) copy-start(f32[1,256]{1,0:T(1,128)} %value_ref.1) | copy-start | bytes 3076
  0.0 10.3 %copy-start.8 = (s32[1,128]{1,0:T(1,128)S(1)}, s32[1,128]{1,0:T(1,128)}, u32[]{:S(2)}) copy-start(s32[1,128]{1,0:T(1,128)} %cnt_ref.1) | copy-start | bytes 1540
  0.0 1.8 %copy-start = (bf16[32,160,2,128]{3,2,1,0:T(2,128)(2,1)S(1)}, bf16[32,160,2,128]{3,2,1,0:T(2,128)(2,1)}, u32[]{:S(2)}) copy-start(bf16[32,160,2,128]{3,2,1,0:T(2,128)(2,1)} %param.11) | copy-start | bytes 7864324
  1.8 2.4 %copy-start.1 = (f32[4,2,128]{2,1,0:T(2,128)S(1)}, f32[4,2,128]{2,1,0:T(2,128)}, u32[]{:S(2)}) copy-start(f32[4,2,128]{2,1,0:T(2,128)} %param.18) | copy-start | bytes 12292
  1.8 2.4 %copy-start.2 = (f32[4,2,128]{2,1,0:T(2,128)S(1)}, f32[4,2,128]{2,1,0:T(2,128)}, u32[]{:S(2)}) copy-start(f32[4,2,128]{2,1,0:T(2,128)} %param.19) | copy-start | bytes 12292
  1.8 2.4 %copy-start.4 = (f32[1,256]{1,0:T(1,128)S(1)}, f32[1,256]{1,0:T(1,128)}, u32[]{:S(2)}) copy-start(f32[1,256]{1,0:T(1,128)} %error_ref.1) | copy-start | bytes 3076
  1.8 2.4 %copy-start.5 = (s32[1,256]{1,0:T(1,128)S(1)}, s32[1,256]{1,0:T(1,128)}, u32[]{:S(2)}) copy-start(s32[1,256]{1,0:T(1,128)} %cell_ref.1) | copy-start | bytes 3076
  1.8 2.4 %copy-start.6 = (s32[1,256]{1,0:T(1,128)S(1)}, s32[1,256]{1,0:T(1,128)}, u32[]{:S(2)}) copy-start(s32[1,256]{1,0:T(1,128)} %species_ref.1) | copy-start | bytes 3076
  1.8 8.4 %copy-start.10 = (f32[40]{0:T(128)S(1)}, f32[40]{0:T(128)}, u32[]{:S(2)}) copy-start(f32[40]{0:T(128)} %param.20) | copy-start | bytes 484
  1.8 8.5 %copy-start.7 = (s32[1,128,32]{1,2,0:T(8,128)S(1)}, s32[1,128,32]{1,2,0:T(8,128)}, u32[]{:S(2)}) copy-start(s32[1,128,32]{1,2,0:T(8,128)} %param.16) | copy-start | bytes 49156
  9.6 24.2 %collective-permute-start = (bf16[32,112,128]{2,1,0:T(8,128)(2,1)}, bf16[32,112,128]{2,1,0:T(8,128)(2,1)S(1)}, u32[]{:S(2)}, u32[]{:S(2)}) collective-permute-start(bf16[32,112,128]{2,1,0:T(8,128)(2,1)} %get-tuple-element.20), channel_id=1, source_target_pairs={{0,16},{16,0},{1,17},{17,1},{2,18},{18,2},{3,19},{19,3},{4,20},{20... | collective-permute-start | bytes 2752520 | tf_op jit(solution)/shard_map/ppermute | solution.py:913
  10.4 23.2 %copy-start.9 = (f32[2,128]{1,0:T(2,128)S(1)}, f32[2,128]{1,0:T(2,128)}, u32[]{:S(2)}) copy-start(f32[2,128]{1,0:T(2,128)} %param.21) | copy-start | bytes 3076

commit v6 on v5

--- a/solution.py
+++ b/solution.py
@@ -15,9 +15,9 @@
 GROUP = 8
 PITCH = 40
 WIDTH = 16
-LAG = 6
+LAG = 8
 RELAY = 3
-LATE = 3
+LATE = 2
 QUAD = 4
 UNROLL = 8
 INTERPRET = False
@@ -484,7 +484,7 @@
 def finish_kernel(
     slots, width,
     mine_ref, other_ref, theirs_ref, dev_ref, mix_ref, keep_ref, edge_ref, loss_ref, out_ref,
-    rows, away, south, north, held_ref, late_ref, anomaly, mapped, mean_ref, coef, weave,
+    rows, away, south, north, held_ref, late_ref, values, mapped, mean_ref, coef, weave,
     away_sent, away_come, edge_sent, edge_come, held_sent, held_come, late_sent, late_come,
 ):
     share, fields, _ = mine_ref.shape
@@ -627,10 +627,10 @@
         def fill(load, base):
             def one(i, total):
                 value = load(i).astype(jnp.float32)
-                anomaly[base + i] = value
+                values[base + i] = value
                 return total + value
 
-            return lax.fori_loop(0, share, one, zero, unroll=4)
+            return lax.fori_loop(0, share, one, zero, unroll=8)
 
         mean_ref[...] = fill(lambda i: mine_ref[i, cut, :], 0)
 
@@ -643,14 +643,7 @@
             follow(q - early).wait_recv()
             mean_ref[...] += fill(lambda i: late_ref[q - early, i], share)
 
-        mean = mean_ref[...] * (1.0 / members)
-        mean_ref[...] = mean
-
-        def subtract(i, carry):
-            anomaly[i] = anomaly[i] - mean
-            return carry
-
-        lax.fori_loop(0, members, subtract, 0, unroll=8)
+        mean_ref[...] = (1.0 - keep_ref[...]) * (mean_ref[...] * (1.0 / members))
 
         def to_mapped(first, sums):
             for r in range(group):
@@ -658,14 +651,14 @@
 
         lane_product(
             lambda i, first, r: dev_ref[pl.ds(i * PITCH + first + r, 1), :],
-            lambda i: anomaly[i], members, slots, width, to_mapped, group=group,
+            lambda i: values[i], members, slots, width, to_mapped, group=group,
         )
         for part in (0, 1):
             base = part * share
 
             def to_out(first, sums, base=base, part=part):
                 for r in range(group):
-                    held = mean_ref[...] + keep_ref[...] * anomaly[base + first + r]
+                    held = mean_ref[...] + keep_ref[...] * values[base + first + r]
                     value = (held + sums[r]).astype(jnp.bfloat16)
                     if part:
                         away[q, first + r] = value

time: 100 us -> 98.9 us (0.989)
  the two profiles are of different devices: /device:TPU:15 before, /device:TPU:17 now
where the time goes in v6:
time: 98.9 us; the launch traced here: 97.4 us
  Pallas kernels  92.6 us (94%)
  local copies, waits for them, and re-layouts  3.45 us (3%)
    pallas_call x1, Pallas kernels, finish(): pl.pallas_call(functools.partial(finish_kernel, slots, width), in_specs=[...  61.1 us
    pallas_call x1, Pallas kernels, solve_cells(): pl.pallas_call(functools.partial(weights_kernel, members, NEWTON, LOC), g...  23.2 us
    pallas_call x1, Pallas kernels, prepare(): pl.pallas_call(functools.partial(prep_kernel, rows, species), in_specs=[v...  6 us
    unnamed x23, local copies, waits for them, and re-layouts  3.3 us
    pallas_call x1, Pallas kernels, separate(): pl.pallas_call(functools.partial(split_kernel, rows, levels), grid=(share...  2.36 us
  transfers between devices with their start and end apart: 1, of which 0 were waited for; matrix products, arithmetic and copies ran while one was open for 0% of the time, Pallas kernels for 24%

profile of v6, /device:TPU:17, one launch (start us, length us, event | category | flops | bytes accessed | tf_op | source)
XLA Modules:
  0.0 97.4 jit_solution(5942282597423060436)
XLA Ops:
  0.0 1.8 %copy-done = bf16[32,160,2,128]{3,2,1,0:T(2,128)(2,1)S(1)} copy-done((bf16[32,160,2,128]{3,2,1,0:T(2,128)(2,1)S(1)}, bf16[32,160,2,128]{3,2,1,0:T(2,128)(2,1)}, u32[]{:S(2)}) %copy-start) | copy-done | bytes 2621464
  1.8 0.0 copy-start.6
  1.8 0.0 copy-start.10
  1.8 0.0 copy-start.7
  1.8 2.4 %shard_map.109 = (bf16[32,160,128]{2,1,0:T(8,128)(2,1)S(1)}, bf16[32,128,128]{2,1,0:T(8,128)(2,1)}, bf16[32,32,128]{2,1,0:T(8,128)(2,1)S(1)}, bf16[32,80,128]{2,1,0:T(8,128)(2,1)S(1)}) custom-call(bf16[10240,128]{1,0:T(8,128)(2,1)S(1)} %bitcast.9), custom_call_target="tpu_custom_call" | custom-call | flops 10000000 | bytes 6000000 | tf_op jit(solution)/shard_map/pallas_call | solution.py:286
  4.2 0.0 copy-done.3
  4.2 0.0 copy-done.1
  4.2 0.0 copy-done.2
  4.2 0.0 copy-done.4
  4.2 0.0 copy-done.5
  4.2 0.0 copy-done.6
  4.2 6.0 %shard_map.110 = (f32[72,768]{1,0:T(8,128)S(1)}, f32[3,16,256]{2,1,0:T(8,128)S(1)}) custom-call(bf16[32,80,128]{2,1,0:T(8,128)(2,1)S(1)} %get-tuple-element.18.lowest_ref, f32[1,256]{1,0:T(1,128)S(1)} %copy-done.3, f32[1,256]{1,0:T(1,128)S(1)} %copy-done.4, s32[1,256]{1,0:T(1,128)S(1)} %copy-done.5, s32[1,256]{1,0:T(1,128)S(1)} %copy-done.6, ...), custom_call_target="tpu_custom_call" | custom-call | flops 100000000 | bytes 1000000 | tf_op jit(solution)/shard_map/pallas_call | solution.py:413
  10.2 0.9 collective-permute-start
  11.1 0.0 copy-done.10
  11.2 0.1 broadcast_in_dim.33
  11.3 0.0 copy-done.8
  11.3 0.0 copy-start.9
  11.3 23.2 %shard_map.111 = (f32[2560,128]{1,0:T(8,128)S(1)}, f32[2048,128]{1,0:T(8,128)S(1)}, f32[1,128]{1,0:T(1,128)S(1)}) custom-call(f32[72,768]{1,0:T(8,128)S(1)} %get-tuple-element.22.pool_ref, s32[32,128]{1,0:T(8,128)S(1)} %bitcast.12, s32[1,128]{1,0:T(1,128)S(1)} %copy-done.8, f32[1,128]{1,0:T(1,128)S(1)} %get-tuple-element.28.row_ref, ...), custom_call_target="tpu_custom_call" | custom-call | flops 2000000000 | bytes 200000000 | tf_op jit(solution)/shard_map/pallas_call | solution.py:239
  34.5 0.0 copy-done.9
  34.5 0.1 multiply_exponential_fusion
  34.6 0.1 broadcast_select_fusion.loss_ref
  34.7 0.0 collective-permute-done.other_ref
  34.8 61.1 %shard_map.112 = bf16[10240,128]{1,0:T(8,128)(2,1)S(1)} custom-call(bf16[32,160,128]{2,1,0:T(8,128)(2,1)S(1)} %get-tuple-element.16.mine_ref, bf16[32,128,128]{2,1,0:T(8,128)(2,1)S(1)} %collective-permute-done.other_ref, bf16[32,32,128]{2,1,0:T(8,128)(2,1)S(1)} %get-tuple-element.21.theirs_ref, f32[2560,128]{1,0:T(8,128)S(1)} %get-tuple-element.23.dev_ref, ...), custom_call_target="tpu_custom_call" | custom-call | flops 1000000000 | bytes 10000000 | tf_op jit(solution)/shard_map/pallas_call | solution.py:768
  95.9 1.5 %copy.13 = bf16[32,160,2,128]{3,2,1,0:T(2,128)(2,1)} copy(bf16[32,160,2,128]{3,2,1,0:T(2,128)(2,1)S(1)} %bitcast.8) | data formatting | bytes 5242880
  (13 shorter events, 0.1 us)
Async XLA Ops:
  0.0 4.2 %copy-start.3 = (f32[1,256]{1,0:T(1,128)S(1)}, f32[1,256]{1,0:T(1,128)}, u32[]{:S(2)}) copy-start(f32[1,256]{1,0:T(1,128)} %value_ref.1) | copy-start | bytes 3076
  0.0 11.3 %copy-start.8 = (s32[1,128]{1,0:T(1,128)S(1)}, s32[1,128]{1,0:T(1,128)}, u32[]{:S(2)}) copy-start(s32[1,128]{1,0:T(1,128)} %cnt_ref.1) | copy-start | bytes 1540
  0.0 1.8 %copy-start = (bf16[32,160,2,128]{3,2,1,0:T(2,128)(2,1)S(1)}, bf16[32,160,2,128]{3,2,1,0:T(2,128)(2,1)}, u32[]{:S(2)}) copy-start(bf16[32,160,2,128]{3,2,1,0:T(2,128)(2,1)} %param.11) | copy-start | bytes 7864324
  1.8 2.4 %copy-start.1 = (f32[4,2,128]{2,1,0:T(2,128)S(1)}, f32[4,2,128]{2,1,0:T(2,128)}, u32[]{:S(2)}) copy-start(f32[4,2,128]{2,1,0:T(2,128)} %param.18) | copy-start | bytes 12292
  1.8 2.4 %copy-start.2 = (f32[4,2,128]{2,1,0:T(2,128)S(1)}, f32[4,2,128]{2,1,0:T(2,128)}, u32[]{:S(2)}) copy-start(f32[4,2,128]{2,1,0:T(2,128)} %param.19) | copy-start | bytes 12292
  1.8 2.4 %copy-start.4 = (f32[1,256]{1,0:T(1,128)S(1)}, f32[1,256]{1,0:T(1,128)}, u32[]{:S(2)}) copy-start(f32[1,256]{1,0:T(1,128)} %error_ref.1) | copy-start | bytes 3076
  1.8 2.4 %copy-start.5 = (s32[1,256]{1,0:T(1,128)S(1)}, s32[1,256]{1,0:T(1,128)}, u32[]{:S(2)}) copy-start(s32[1,256]{1,0:T(1,128)} %cell_ref.1) | copy-start | bytes 3076
  1.8 2.4 %copy-start.6 = (s32[1,256]{1,0:T(1,128)S(1)}, s32[1,256]{1,0:T(1,128)}, u32[]{:S(2)}) copy-start(s32[1,256]{1,0:T(1,128)} %species_ref.1) | copy-start | bytes 3076
  1.8 9.3 %copy-start.10 = (f32[40]{0:T(128)S(1)}, f32[40]{0:T(128)}, u32[]{:S(2)}) copy-start(f32[40]{0:T(128)} %param.20) | copy-start | bytes 484
  1.8 9.5 %copy-start.7 = (s32[1,128,32]{1,2,0:T(8,128)S(1)}, s32[1,128,32]{1,2,0:T(8,128)}, u32[]{:S(2)}) copy-start(s32[1,128,32]{1,2,0:T(8,128)} %param.16) | copy-start | bytes 49156
  10.2 24.5 %collective-permute-start = (bf16[32,128,128]{2,1,0:T(8,128)(2,1)}, bf16[32,128,128]{2,1,0:T(8,128)(2,1)S(1)}, u32[]{:S(2)}, u32[]{:S(2)}) collective-permute-start(bf16[32,128,128]{2,1,0:T(8,128)(2,1)} %get-tuple-element.20), channel_id=1, source_target_pairs={{0,16},{16,0},{1,17},{17,1},{2,18},{18,2},{3,19},{19,3},{4,20},{20... | collective-permute-start | bytes 3145736 | tf_op jit(solution)/shard_map/ppermute | solution.py:906
  11.3 23.2 %copy-start.9 = (f32[2,128]{1,0:T(2,128)S(1)}, f32[2,128]{1,0:T(2,128)}, u32[]{:S(2)}) copy-start(f32[2,128]{1,0:T(2,128)} %param.21) | copy-start | bytes 3076

commit v7 on v6

--- a/solution.py
+++ b/solution.py
@@ -299,7 +299,7 @@
 def prep_kernel(
     rows, species,
     lowest_ref, value_ref, error_ref, cell_ref, species_ref, courant_x_ref, courant_y_ref,
-    pool_ref, edge_ref, found, block, facts_ref, land, land_facts, send_sems, recv_sems, facts_sent, facts_come,
+    pool_ref, edge_ref, found, block, facts_ref, wind, land, land_facts, send_sems, recv_sems, facts_sent, facts_come,
 ):
     share = lowest_ref.shape[0]
     observed = value_ref.shape[1]
@@ -334,10 +334,11 @@
     for n, fact in enumerate(facts):
         facts_ref[pl.ds(n, 1), :] = fact
     for n, courant in enumerate((courant_x_ref, courant_y_ref)):
+        wind[n, pl.ds(0, rows * levels), :] = courant[...]
         for copy in range(GROUP // levels):
             for r in range(rows):
                 start = (n + 1) * GROUP + copy * levels
-                facts_ref[pl.ds(start, levels), pl.ds(r * LANES, LANES)] = courant[pl.ds(r, levels, stride=rows), :]
+                facts_ref[pl.ds(start, levels), pl.ds(r * LANES, LANES)] = wind[n, pl.ds(r, levels, stride=rows), :]
     hot = jnp.where(lax.broadcasted_iota(jnp.int32, (LANES, observed), 0) == column, 1.0, 0.0).astype(jnp.bfloat16)
     wanted = lax.broadcasted_iota(jnp.int32, (rows * species, observed), 0) == row * species + species_ref[...]
 
@@ -349,7 +350,7 @@
         return carry
 
     lax.fori_loop(0, share // UNROLL, look, 0)
-    block[...] = found[...].astype(jnp.bfloat16)
+    block[...] = found[pl.ds(0, share), :].astype(jnp.bfloat16)
 
     greeted = 1 + 2 * exists(-1).astype(jnp.int32) + 2 * exists(1).astype(jnp.int32)
     pl.semaphore_wait(barrier, greeted)
@@ -364,7 +365,7 @@
 
     def copy_facts(step):
         return pltpu.make_async_remote_copy(
-            src_ref=facts_ref, dst_ref=land_facts.at[1 - step],
+            src_ref=facts_ref.at[pl.ds(0, 3 * GROUP)], dst_ref=land_facts.at[1 - step],
             send_sem=facts_sent.at[1 - step], recv_sem=facts_come.at[1 - step],
             device_id=(me, place + step), device_id_type=pl.DeviceIdType.MESH,
         )
@@ -389,8 +390,8 @@
     line = lax.broadcasted_iota(jnp.int32, (GROUP, observed), 0)
     for part in range(3):
         lanes = pl.ds(part * observed, observed)
-        own = found[...] if part == 1 else land[part, 0].astype(jnp.float32)
-        facts = (facts_ref if part == 1 else land_facts.at[part])[...]
+        own = found[pl.ds(0, share), :] if part == 1 else land[part, 0].astype(jnp.float32)
+        facts = facts_ref[pl.ds(0, 3 * GROUP), :] if part == 1 else land_facts[part]
         pool_ref[pl.ds(0, share), lanes] = own
         pool_ref[pl.ds(share, share), lanes] = land[part, 1].astype(jnp.float32)
         pool_ref[pl.ds(2 * share, GROUP), lanes] = facts[:GROUP] + jnp.where(
@@ -419,9 +420,10 @@
             jax.ShapeDtypeStruct((3, 2 * GROUP, observed), jnp.float32),
         ],
         scratch_shapes=[
-            pltpu.VMEM((share, observed), jnp.float32),
+            pltpu.VMEM((share + GROUP, observed), jnp.float32),
             pltpu.VMEM((share, observed), jnp.bfloat16),
-            pltpu.VMEM((3 * GROUP, observed), jnp.float32),
+            pltpu.VMEM((4 * GROUP, observed), jnp.float32),
+            pltpu.VMEM((2, 4 * GROUP, LANES), jnp.float32),
             pltpu.VMEM((3, 2, share, observed), jnp.bfloat16),
             pltpu.VMEM((3, 3 * GROUP, observed), jnp.float32),
             pltpu.SemaphoreType.DMA((5,)),
@@ -868,6 +870,7 @@
     per_dev = tile_cells // groups
     paired = groups == 2 and tile_rows == 2 and columns == LANES
     paired = paired and GROUP % levels == 0 and fields % WIDTH == 0 and fields > 2 * LATE * WIDTH and species % GROUP == 0
+    paired = paired and tile_rows * levels <= GROUP
     paired = paired and local_members % UNROLL == 0
     swap = [(0, 1), (1, 0)]
 

time: 98.9 us -> 98.9 us (level)
  no operation moved by 1% of the time
where the time goes in v7:
time: 98.9 us; the launch traced here: 97.4 us
  Pallas kernels  92.6 us (94%)
  local copies, waits for them, and re-layouts  3.45 us (3%)
    pallas_call x1, Pallas kernels, finish(): pl.pallas_call(functools.partial(finish_kernel, slots, width), in_specs=[...  61.1 us
    pallas_call x1, Pallas kernels, solve_cells(): pl.pallas_call(functools.partial(weights_kernel, members, NEWTON, LOC), g...  23.2 us
    pallas_call x1, Pallas kernels, prepare(): pl.pallas_call(functools.partial(prep_kernel, rows, species), in_specs=[v...  6 us
    unnamed x23, local copies, waits for them, and re-layouts  3.3 us
    pallas_call x1, Pallas kernels, separate(): pl.pallas_call(functools.partial(split_kernel, rows, levels), grid=(share...  2.36 us
  transfers between devices with their start and end apart: 1, of which 0 were waited for; matrix products, arithmetic and copies ran while one was open for 0% of the time, Pallas kernels for 24%

profile of v7, /device:TPU:17, one launch (start us, length us, event | category | flops | bytes accessed | tf_op | source)
XLA Modules:
  0.0 97.4 jit_solution(17496064939738299406)
XLA Ops:
  0.0 1.8 %copy-done = bf16[32,160,2,128]{3,2,1,0:T(2,128)(2,1)S(1)} copy-done((bf16[32,160,2,128]{3,2,1,0:T(2,128)(2,1)S(1)}, bf16[32,160,2,128]{3,2,1,0:T(2,128)(2,1)}, u32[]{:S(2)}) %copy-start) | copy-done | bytes 2621464
  1.8 0.0 copy-start.6
  1.8 0.0 copy-start.10
  1.8 0.0 copy-start.7
  1.8 2.4 %shard_map.109 = (bf16[32,160,128]{2,1,0:T(8,128)(2,1)S(1)}, bf16[32,128,128]{2,1,0:T(8,128)(2,1)}, bf16[32,32,128]{2,1,0:T(8,128)(2,1)S(1)}, bf16[32,80,128]{2,1,0:T(8,128)(2,1)S(1)}) custom-call(bf16[10240,128]{1,0:T(8,128)(2,1)S(1)} %bitcast.9), custom_call_target="tpu_custom_call" | custom-call | flops 10000000 | bytes 6000000 | tf_op jit(solution)/shard_map/pallas_call | solution.py:286
  4.2 0.0 copy-done.3
  4.2 0.0 copy-done.1
  4.2 0.0 copy-done.2
  4.2 0.0 copy-done.4
  4.2 0.0 copy-done.5
  4.2 0.0 copy-done.6
  4.2 6.0 %shard_map.110 = (f32[72,768]{1,0:T(8,128)S(1)}, f32[3,16,256]{2,1,0:T(8,128)S(1)}) custom-call(bf16[32,80,128]{2,1,0:T(8,128)(2,1)S(1)} %get-tuple-element.18.lowest_ref, f32[1,256]{1,0:T(1,128)S(1)} %copy-done.3, f32[1,256]{1,0:T(1,128)S(1)} %copy-done.4, s32[1,256]{1,0:T(1,128)S(1)} %copy-done.5, s32[1,256]{1,0:T(1,128)S(1)} %copy-done.6, ...), custom_call_target="tpu_custom_call" | custom-call | flops 100000000 | bytes 1000000 | tf_op jit(solution)/shard_map/pallas_call | solution.py:414
  10.2 0.9 collective-permute-start
  11.1 0.0 copy-done.10
  11.2 0.1 broadcast_in_dim.33
  11.3 0.0 copy-done.8
  11.3 0.0 copy-start.9
  11.3 23.2 %shard_map.111 = (f32[2560,128]{1,0:T(8,128)S(1)}, f32[2048,128]{1,0:T(8,128)S(1)}, f32[1,128]{1,0:T(1,128)S(1)}) custom-call(f32[72,768]{1,0:T(8,128)S(1)} %get-tuple-element.22.pool_ref, s32[32,128]{1,0:T(8,128)S(1)} %bitcast.12, s32[1,128]{1,0:T(1,128)S(1)} %copy-done.8, f32[1,128]{1,0:T(1,128)S(1)} %get-tuple-element.28.row_ref, ...), custom_call_target="tpu_custom_call" | custom-call | flops 2000000000 | bytes 200000000 | tf_op jit(solution)/shard_map/pallas_call | solution.py:239
  34.5 0.0 copy-done.9
  34.5 0.1 multiply_exponential_fusion
  34.6 0.1 broadcast_select_fusion.loss_ref
  34.7 0.0 collective-permute-done.other_ref
  34.8 61.1 %shard_map.112 = bf16[10240,128]{1,0:T(8,128)(2,1)S(1)} custom-call(bf16[32,160,128]{2,1,0:T(8,128)(2,1)S(1)} %get-tuple-element.16.mine_ref, bf16[32,128,128]{2,1,0:T(8,128)(2,1)S(1)} %collective-permute-done.other_ref, bf16[32,32,128]{2,1,0:T(8,128)(2,1)S(1)} %get-tuple-element.21.theirs_ref, f32[2560,128]{1,0:T(8,128)S(1)} %get-tuple-element.23.dev_ref, ...), custom_call_target="tpu_custom_call" | custom-call | flops 1000000000 | bytes 10000000 | tf_op jit(solution)/shard_map/pallas_call | solution.py:770
  95.9 1.5 %copy.13 = bf16[32,160,2,128]{3,2,1,0:T(2,128)(2,1)} copy(bf16[32,160,2,128]{3,2,1,0:T(2,128)(2,1)S(1)} %bitcast.8) | data formatting | bytes 5242880
  (13 shorter events, 0.1 us)
Async XLA Ops:
  0.0 4.2 %copy-start.3 = (f32[1,256]{1,0:T(1,128)S(1)}, f32[1,256]{1,0:T(1,128)}, u32[]{:S(2)}) copy-start(f32[1,256]{1,0:T(1,128)} %value_ref.1) | copy-start | bytes 3076
  0.0 11.3 %copy-start.8 = (s32[1,128]{1,0:T(1,128)S(1)}, s32[1,128]{1,0:T(1,128)}, u32[]{:S(2)}) copy-start(s32[1,128]{1,0:T(1,128)} %cnt_ref.1) | copy-start | bytes 1540
  0.0 1.8 %copy-start = (bf16[32,160,2,128]{3,2,1,0:T(2,128)(2,1)S(1)}, bf16[32,160,2,128]{3,2,1,0:T(2,128)(2,1)}, u32[]{:S(2)}) copy-start(bf16[32,160,2,128]{3,2,1,0:T(2,128)(2,1)} %param.11) | copy-start | bytes 7864324
  1.8 2.4 %copy-start.1 = (f32[4,2,128]{2,1,0:T(2,128)S(1)}, f32[4,2,128]{2,1,0:T(2,128)}, u32[]{:S(2)}) copy-start(f32[4,2,128]{2,1,0:T(2,128)} %param.18) | copy-start | bytes 12292
  1.8 2.4 %copy-start.2 = (f32[4,2,128]{2,1,0:T(2,128)S(1)}, f32[4,2,128]{2,1,0:T(2,128)}, u32[]{:S(2)}) copy-start(f32[4,2,128]{2,1,0:T(2,128)} %param.19) | copy-start | bytes 12292
  1.8 2.4 %copy-start.4 = (f32[1,256]{1,0:T(1,128)S(1)}, f32[1,256]{1,0:T(1,128)}, u32[]{:S(2)}) copy-start(f32[1,256]{1,0:T(1,128)} %error_ref.1) | copy-start | bytes 3076
  1.8 2.4 %copy-start.5 = (s32[1,256]{1,0:T(1,128)S(1)}, s32[1,256]{1,0:T(1,128)}, u32[]{:S(2)}) copy-start(s32[1,256]{1,0:T(1,128)} %cell_ref.1) | copy-start | bytes 3076
  1.8 2.4 %copy-start.6 = (s32[1,256]{1,0:T(1,128)S(1)}, s32[1,256]{1,0:T(1,128)}, u32[]{:S(2)}) copy-start(s32[1,256]{1,0:T(1,128)} %species_ref.1) | copy-start | bytes 3076
  1.8 9.3 %copy-start.10 = (f32[40]{0:T(128)S(1)}, f32[40]{0:T(128)}, u32[]{:S(2)}) copy-start(f32[40]{0:T(128)} %param.20) | copy-start | bytes 484
  1.8 9.5 %copy-start.7 = (s32[1,128,32]{1,2,0:T(8,128)S(1)}, s32[1,128,32]{1,2,0:T(8,128)}, u32[]{:S(2)}) copy-start(s32[1,128,32]{1,2,0:T(8,128)} %param.16) | copy-start | bytes 49156
  10.2 24.5 %collective-permute-start = (bf16[32,128,128]{2,1,0:T(8,128)(2,1)}, bf16[32,128,128]{2,1,0:T(8,128)(2,1)S(1)}, u32[]{:S(2)}, u32[]{:S(2)}) collective-permute-start(bf16[32,128,128]{2,1,0:T(8,128)(2,1)} %get-tuple-element.20), channel_id=1, source_target_pairs={{0,16},{16,0},{1,17},{17,1},{2,18},{18,2},{3,19},{19,3},{4,20},{20... | collective-permute-start | bytes 3145736 | tf_op jit(solution)/shard_map/ppermute | solution.py:909
  11.3 23.2 %copy-start.9 = (f32[2,128]{1,0:T(2,128)S(1)}, f32[2,128]{1,0:T(2,128)}, u32[]{:S(2)}) copy-start(f32[2,128]{1,0:T(2,128)} %param.21) | copy-start | bytes 3076
